TPU v7x, 32 devices: a whole 2x2x4 slice. The times are simulated.
32 devices in a mesh: gx: 8 (over z, x), gy: 4 (over y, core).
Axes of the slice: x: 2, y: 2, z: 4, core: 2. Of those that a mesh axis runs over, the one named last changes fastest.
Arguments:
- orbitals: bfloat16 [20000, 200], P('gx'), may hold values from -6 to 6
- projector: bfloat16 [6016, 20000], P('gy', 'gx'), may hold values from -0.0390625 to 0.0390625
- integrals: bfloat16 [8, 6016, 6016], P('gx', 'gy'), may hold values from -1 to 1
Outputs:
- exchange_matrix: float32 [6016, 6016], P('gx', 'gy')
- exchange_orbitals: float32 [20000, 200], P('gx', 'gy')
- energy_mean: float32 [], replicated
- trace_mean: float32 [], replicated
All inputs are finite; a program needn't handle non-finite values.
Results may differ from a plain program's by a relative error of at most 0.008.
Values may be sent and summed in bfloat16 or wider, within the bound.
A program may use at most 128 MiB of HBM per device.

v0:
```python
import functools

import jax
import jax.numpy as jnp
from jax import lax
from jax.experimental import pallas as pl
from jax.experimental.pallas import tpu as pltpu
from jax.sharding import PartitionSpec as P

MESH = pl.DeviceIdType.MESH
LIMIT = 60 * 1024 * 1024


def factor(size):
    inner = 1
    while inner * inner * 4 <= size:
        inner *= 2
    return size // inner, inner


def up(value, unit):
    return -(-value // unit) * unit


def remote(src, dst, send, recv, dev):
    return pltpu.make_async_remote_copy(
        src_ref=src, dst_ref=dst, send_sem=send, recv_sem=recv, device_id=dev, device_id_type=MESH
    )


def greet(size_x, size_y):
    gx, gy = lax.axis_index("gx"), lax.axis_index("gy")
    barrier = pltpu.get_barrier_semaphore()

    def hello(step, carry):
        other = lax.rem(gx * size_y + gy + step, size_x * size_y)
        pl.semaphore_signal(
            barrier, inc=1, device_id=(other // size_y, lax.rem(other, size_y)), device_id_type=MESH
        )
        return carry

    lax.fori_loop(1, size_x * size_y, hello, 0)
    pl.semaphore_wait(barrier, size_x * size_y - 1)


def reduce_gather_kernel(
    size_x, size_y, wide, part, out, landing, send_a, recv_a, send_z, recv_z, send_x, recv_x, send_y, recv_y, send_c, recv_c
):
    gx, gy = lax.axis_index("gx"), lax.axis_index("gy")
    num_z, num_x = factor(size_x)
    z, x = gx // num_x, lax.rem(gx, num_x)
    num_y = size_y // 2
    y, c = gy // 2, lax.rem(gy, 2)
    greet(size_x, size_y)
    outgoing = []
    for d in range(1, size_x):
        to = lax.rem(gx + d, size_x)
        copy = remote(part.at[to], landing.at[d], send_a.at[d], recv_a.at[d], (to, gy))
        copy.start()
        outgoing.append(copy)
    total = part[gx].astype(jnp.float32)
    for d in range(1, size_x):
        outgoing[d - 1].wait_recv()
        total = total + landing[d].astype(jnp.float32)
    row = gy if wide else 0
    out[row, gx] = total.astype(out.dtype)
    pending = []

    def piece(group, who):
        return out.at[group, who]

    def to_core(group, who, slot):
        if wide:
            copy = remote(piece(group, who), piece(group, who), send_c.at[slot], recv_c.at[slot], (gx, gy + 1 - 2 * c))
            copy.start()
            pending.append(copy)

    def to_y(group, who, slot):
        if wide:
            for d in range(1, num_y):
                there = lax.rem(y + d, num_y)
                copy = remote(
                    piece(group, who), piece(group, who), send_y.at[slot, d], recv_y.at[slot, d], (gx, there * 2 + c)
                )
                copy.start()
                pending.append(copy)

    for d in range(1, num_z):
        to = lax.rem(z + d, num_z) * num_x + x
        copy = remote(piece(row, gx), piece(row, gx), send_z.at[d], recv_z.at[d], (to, gy))
        copy.start()
        pending.append(copy)
    for d in range(num_z):
        src_z = lax.rem(z - d + num_z, num_z)
        who = src_z * num_x + x
        if d > 0:
            remote(piece(row, who), piece(row, who), send_z.at[d], recv_z.at[d], (gx, gy)).wait_recv()
        for e in range(1, num_x):
            to = z * num_x + lax.rem(x + e, num_x)
            copy = remote(piece(row, who), piece(row, who), send_x.at[d, e], recv_x.at[d, e], (to, gy))
            copy.start()
            pending.append(copy)
        to_y(row, who, d * num_x)
        to_core(row, who, d * num_x)
    for d in range(num_z):
        src_z = lax.rem(z - d + num_z, num_z)
        for e in range(1, num_x):
            who = src_z * num_x + lax.rem(x - e + num_x, num_x)
            remote(piece(row, who), piece(row, who), send_x.at[d, e], recv_x.at[d, e], (gx, gy)).wait_recv()
            to_y(row, who, d * num_x + e)
            to_core(row, who, d * num_x + e)
    if wide:
        for d in range(num_z):
            for e in range(num_x):
                who = lax.rem(z - d + num_z, num_z) * num_x + lax.rem(x - e + num_x, num_x)
                slot = d * num_x + e
                for f in range(1, num_y):
                    group = lax.rem(y - f + num_y, num_y) * 2 + c
                    remote(piece(group, who), piece(group, who), send_y.at[slot, f], recv_y.at[slot, f], (gx, gy)).wait_recv()
                    to_core(group, who, f * size_x + slot)
        for d in range(num_z):
            for e in range(num_x):
                who = lax.rem(z - d + num_z, num_z) * num_x + lax.rem(x - e + num_x, num_x)
                for f in range(num_y):
                    group = lax.rem(y - f + num_y, num_y) * 2 + 1 - c
                    slot = f * size_x + d * num_x + e
                    remote(piece(group, who), piece(group, who), send_c.at[slot], recv_c.at[slot], (gx, gy)).wait_recv()
    for copy in outgoing:
        copy.wait_send()
    for copy in pending:
        copy.wait_send()


def reduce_gather(part, size_x, size_y, wide, number):
    rows, cols = part.shape
    chunk = up(-(-rows // size_x), 16)
    padded = jnp.pad(part.astype(jnp.bfloat16), ((0, chunk * size_x - rows), (0, 0)))
    padded = padded.reshape(size_x, chunk, cols)
    num_z, num_x = factor(size_x)
    groups = size_y if wide else 1
    dma = pltpu.SemaphoreType.DMA
    out = pl.pallas_call(
        functools.partial(reduce_gather_kernel, size_x, size_y, wide),
        out_shape=jax.ShapeDtypeStruct((groups, size_x, chunk, cols), jnp.bfloat16),
        in_specs=[pl.BlockSpec(memory_space=pltpu.VMEM)],
        out_specs=pl.BlockSpec(memory_space=pltpu.VMEM),
        scratch_shapes=[
            pltpu.VMEM((size_x, chunk, cols), jnp.bfloat16),
            dma((size_x,)),
            dma((size_x,)),
            dma((num_z,)),
            dma((num_z,)),
            dma((num_z, num_x)),
            dma((num_z, num_x)),
            dma((size_x, size_y // 2)),
            dma((size_x, size_y // 2)),
            dma((size_x * size_y // 2,)),
            dma((size_x * size_y // 2,)),
        ],
        compiler_params=pltpu.CompilerParams(collective_id=number, has_side_effects=True, vmem_limit_bytes=LIMIT),
    )(padded)
    return out.reshape(groups, size_x * chunk, cols)[:, :rows]


def exchange_kernel(
    size_x, size_y, block, own, stats, out, sums, cols, rows, acc, landing, send_s, recv_s, own_sem, send_u, recv_u, send_d, recv_d, send_x, recv_x, send_y, recv_y, send_c, recv_c, row_sem
):
    gx, gy = lax.axis_index("gx"), lax.axis_index("gy")
    num_z, num_x = factor(size_x)
    z, x = gx // num_x, lax.rem(gx, num_x)
    num_y = size_y // 2
    y, c = gy // 2, lax.rem(gy, 2)
    width = out.shape[1]
    window = rows.shape[2]
    per = size_x // size_y
    root = gx // per
    root_y, root_c = root // 2, lax.rem(root, 2)
    offset = lax.rem(gx, per) * block
    first = pl.multiple_of(jnp.minimum(offset // 128 * 128, cols.shape[2] - window), 128)
    mine = gy == root
    below = (y != root_y) & (c == root_c)
    last = c != root_c
    greet(size_x, size_y)
    mypiece = pltpu.make_async_copy(own, cols.at[gx], own_sem)
    mypiece.start()
    mypiece.wait()
    devices = size_x * size_y
    me = gx * size_y + gy

    def stat_copy(slot, step, to):
        return remote(stats, landing.at[slot], send_s.at[step], recv_s.at[slot], (to // size_y, lax.rem(to, size_y)))

    def upward(k):
        who = jnp.maximum(z - k, 0) * num_x + x
        return remote(cols.at[who], cols.at[who], send_u.at[k], recv_u.at[k], (jnp.minimum(z + 1, num_z - 1) * num_x + x, gy))

    def downward(k):
        who = jnp.minimum(z + k, num_z - 1) * num_x + x
        return remote(cols.at[who], cols.at[who], send_d.at[k], recv_d.at[k], (jnp.maximum(z - 1, 0) * num_x + x, gy))

    def sideways(slot, who, e):
        to = z * num_x + lax.rem(x + e, num_x)
        return remote(cols.at[who], cols.at[who], send_x.at[slot, e], recv_x.at[slot, e], (to, gy))

    def row_y(who, f):
        return remote(
            cols.at[who, :, pl.ds(first, window)], rows.at[who], send_y.at[who, f], recv_y.at[who], (gx, lax.rem(y + f, num_y) * 2 + c)
        )

    def row_c(who, source):
        return remote(source, rows.at[who], send_c.at[who], recv_c.at[who], (gx, gy + 1 - 2 * c))

    def row_own(who):
        return pltpu.make_async_copy(cols.at[who, :, pl.ds(first, window)], rows.at[who], row_sem.at[who])

    def have(who):
        @pl.when(mine)
        def _():
            for f in range(1, num_y):
                row_y(who, f).start()
            row_c(who, cols.at[who, :, pl.ds(first, window)]).start()
            row_own(who).start()

    def spread(slot, who):
        for e in range(1, num_x):
            sideways(slot, who, e).start()
        have(who)

    def add_term(who, fresh):
        @pl.when(mine)
        def _():
            row_own(who).wait()

        @pl.when(below)
        def _():
            row_y(who, 1).wait_recv()
            row_c(who, rows.at[who]).start()

        @pl.when(last)
        def _():
            row_c(who, rows.at[who]).wait_recv()

        for start in range(0, width, 512):
            span = min(512, width - start)
            term = lax.dot_general(
                rows[who], cols[who, :, start:start + span], (((0,), (0,)), ((), ())), preferred_element_type=jnp.float32
            )
            if fresh:
                acc[:, start:start + span] = term
            else:
                acc[:, start:start + span] += term

    def add_terms(k):
        if k == 0:
            add_term(gx, True)

        def one(i, carry):
            src_z = z + jnp.where(i < num_x, -k, k)

            @pl.when((src_z >= 0) & (src_z < num_z))
            def _():
                add_term(src_z * num_x + lax.rem(x + lax.rem(i, num_x), num_x), False)

            return carry

        lax.fori_loop(0 if k else 1, 2 * num_x if k else num_x, one, 0)

    for k in range(num_z):
        if k > 0:
            @pl.when(z >= k)
            def _(k=k):
                who = jnp.maximum(z - k, 0) * num_x + x
                remote(cols.at[who], cols.at[who], send_u.at[k - 1], recv_u.at[k - 1], (gx, gy)).wait_recv()
        if k < num_z - 1:
            @pl.when((z >= k) & (z < num_z - 1))
            def _(k=k):
                upward(k).start()
        if k > 0:
            @pl.when(z + k < num_z)
            def _(k=k):
                who = jnp.minimum(z + k, num_z - 1) * num_x + x
                remote(cols.at[who], cols.at[who], send_d.at[k - 1], recv_d.at[k - 1], (gx, gy)).wait_recv()
        if k < num_z - 1:
            @pl.when((z + k < num_z) & (z > 0))
            def _(k=k):
                downward(k).start()
        for side in ((1, -1) if k else (1,)):
            src_z = z - side * k
            @pl.when((src_z >= 0) & (src_z < num_z))
            def _(src_z=src_z):
                src_z = jnp.clip(src_z, 0, num_z - 1)
                spread(src_z, src_z * num_x + x)
        if k == 0:
            def tell(step, carry):
                stat_copy(me, step, lax.rem(me + step, devices)).start()
                return carry

            lax.fori_loop(1, devices, tell, 0)
        else:
            add_terms(k - 1)
        for side in ((1, -1) if k else (1,)):
            src_z = z - side * k
            @pl.when((src_z >= 0) & (src_z < num_z))
            def _(src_z=src_z):
                src_z = jnp.clip(src_z, 0, num_z - 1)
                for e in range(1, num_x):
                    who = src_z * num_x + lax.rem(x - e + num_x, num_x)
                    sideways(src_z, who, e).wait_recv()
                    have(who)
    add_terms(num_z - 1)

    def hear(step, carry):
        stat_copy(lax.rem(me + step, devices), step, me).wait_recv()
        return carry

    lax.fori_loop(1, devices, hear, 0)
    landing[me] = stats[...]
    sums[...] = jnp.sum(landing[...], axis=0)

    def told(step, carry):
        stat_copy(me, step, me).wait_send()
        return carry

    lax.fori_loop(1, devices, told, 0)
    for i in range(per):
        at = i * block - min(i * block // 128 * 128, cols.shape[2] - window)

        @pl.when(lax.rem(gx, per) == i)
        def _(at=at):
            out[...] = acc[at:at + block, :]

    for k in range(num_z - 1):
        @pl.when((z >= k) & (z < num_z - 1))
        def _(k=k):
            upward(k).wait_send()

        @pl.when((z + k < num_z) & (z > 0))
        def _(k=k):
            downward(k).wait_send()
    for src_z in range(num_z):
        for e in range(1, num_x):
            sideways(src_z, src_z * num_x + x, e).wait_send()

    def drain(who, carry):
        @pl.when(mine)
        def _():
            for f in range(1, num_y):
                row_y(who, f).wait_send()

        @pl.when(mine | below)
        def _():
            row_c(who, rows.at[who]).wait_send()

        return carry

    lax.fori_loop(0, size_x, drain, 0)


def exchange_of(half_t, stats, size_x, size_y, block, number):
    occ, width = half_t.shape
    num_z, num_x = factor(size_x)
    per = size_x // size_y
    padded = up(width, 128)
    window = max(up(i * block % 128 + block, 128) for i in range(per))
    dma = pltpu.SemaphoreType.DMA
    half_t = jnp.pad(half_t, ((0, 0), (0, padded - width)))
    return pl.pallas_call(
        functools.partial(exchange_kernel, size_x, size_y, block),
        out_shape=(jax.ShapeDtypeStruct((block, width), jnp.float32), jax.ShapeDtypeStruct(stats.shape, jnp.float32)),
        in_specs=[pl.BlockSpec(memory_space=pltpu.VMEM)] * 2,
        out_specs=[pl.BlockSpec(memory_space=pltpu.VMEM)] * 2,
        scratch_shapes=[
            pltpu.VMEM((size_x, occ, padded), jnp.bfloat16),
            pltpu.VMEM((size_x, occ, window), jnp.bfloat16),
            pltpu.VMEM((window, width), jnp.float32),
            pltpu.VMEM((size_x * size_y,) + stats.shape, jnp.float32),
            dma((size_x * size_y,)),
            dma((size_x * size_y,)),
            dma(()),
            dma((num_z,)),
            dma((num_z,)),
            dma((num_z,)),
            dma((num_z,)),
            dma((num_z, num_x)),
            dma((num_z, num_x)),
            dma((size_x, size_y // 2)),
            dma((size_x,)),
            dma((size_x,)),
            dma((size_x,)),
            dma((size_x,)),
        ],
        compiler_params=pltpu.CompilerParams(collective_id=number, has_side_effects=True, vmem_limit_bytes=LIMIT),
    )(half_t, stats)


def sum_kernel(size_y, same, part, out, landing, send, recv):
    gx, gy = lax.axis_index("gx"), lax.axis_index("gy")
    barrier = pltpu.get_barrier_semaphore()
    for d in range(1, size_y):
        pl.semaphore_signal(barrier, inc=1, device_id=(gx, lax.rem(gy + d, size_y)), device_id_type=MESH)
    pl.semaphore_wait(barrier, size_y - 1)
    copies = []
    for d in range(1, size_y):
        to = lax.rem(gy + d, size_y)
        copy = remote(part.at[0 if same else to], landing.at[d], send.at[d], recv.at[d], (gx, to))
        copy.start()
        copies.append(copy)
    total = part[0 if same else gy].astype(jnp.float32)
    for d in range(1, size_y):
        copies[d - 1].wait_recv()
        total = total + landing[d].astype(jnp.float32)
    out[...] = total
    for copy in copies:
        copy.wait_send()


def sum_over_y(part, size_y, same, number):
    shape = part.shape[1:]
    dma = pltpu.SemaphoreType.DMA
    return pl.pallas_call(
        functools.partial(sum_kernel, size_y, same),
        out_shape=jax.ShapeDtypeStruct(shape, jnp.float32),
        in_specs=[pl.BlockSpec(memory_space=pltpu.VMEM)],
        out_specs=pl.BlockSpec(memory_space=pltpu.VMEM),
        scratch_shapes=[pltpu.VMEM((size_y,) + shape, part.dtype), dma((size_y,)), dma((size_y,))],
        compiler_params=pltpu.CompilerParams(collective_id=number, has_side_effects=True, vmem_limit_bytes=LIMIT),
    )(part)


def on_device(size_x, size_y, orbitals, projector, integrals):
    part_rows = projector.shape[0]
    partial_value = jnp.dot(projector, orbitals, preferred_element_type=jnp.float32)
    groups = reduce_gather(partial_value, size_x, size_y, True, 1)
    occ = groups.shape[2]
    total_adm = part_rows * size_y
    admm = groups.reshape(total_adm, occ)
    half_t = lax.dot_general(
        admm, integrals[0], (((0,), (1,)), ((), ())), preferred_element_type=jnp.float32
    ).astype(jnp.bfloat16)
    own = lax.dynamic_index_in_dim(groups, lax.axis_index("gy"), 0, keepdims=False)
    mixed_part = jnp.dot(half_t, own, preferred_element_type=jnp.float32)
    mixed = sum_over_y(mixed_part[None], size_y, True, 4)
    wide = half_t.astype(jnp.float32)
    trace_part = jnp.sum(wide * wide)
    energy_part = jnp.sum(mixed * mixed) / size_y
    lane = lax.broadcasted_iota(jnp.int32, (8, 128), 1)
    stats = jnp.where(lane == 0, energy_part, jnp.where(lane == 1, trace_part, 0.0))
    applied_part = lax.dot_general(
        half_t, mixed.astype(jnp.bfloat16), (((0,), (0,)), ((), ())), preferred_element_type=jnp.float32
    )
    applied_low = reduce_gather(applied_part, size_x, size_y, False, 3)[0]
    back_part = lax.dot_general(
        applied_low, projector, (((0,), (0,)), ((), ())), preferred_element_type=jnp.float32
    ).astype(jnp.bfloat16)
    back = sum_over_y(back_part.reshape(size_y, occ // size_y, -1), size_y, False, 5).T
    exchange, sums = exchange_of(half_t, stats, size_x, size_y, total_adm // size_x, 2)
    energy_total, trace_total = sums[0, 0], sums[0, 1]
    energy_mean = -0.5 * energy_total / (total_adm * occ)
    trace_mean = trace_total / total_adm
    return (exchange, back, energy_mean, trace_mean)


def solution(mesh):
    return jax.shard_map(
        functools.partial(on_device, mesh.shape["gx"], mesh.shape["gy"]),
        mesh=mesh,
        in_specs=(P("gx", None), P("gy", "gx"), P("gx", "gy", None)),
        out_specs=(P("gx", "gy"), P("gx", "gy"), P(), P()),
        check_vma=False,
    )
```

profile of v0, /device:TPU:7, one launch (start us, length us, event | category | flops | bytes accessed | tf_op | source)
XLA Modules:
  0.0 262.7 jit_solution(12264888154988860980)
XLA Ops:
  0.6 0.0 copy-start
  0.7 1.2 copy-done
  1.9 4.9 %convolution_convert_fusion.1 = bf16[1504,200]{0,1:T(8,128)(2,1)S(1)} fusion(bf16[1504,2500]{0,1:T(8,128)(2,1)} %param.4, bf16[2500,200]{0,1:T(8,128)(2,1)S(1)} %copy-done), kind=kOutput, calls=%fused_computation.3 | convolution fusion | flops 1504300800 | bytes 9121600 | tf_op jit(solution)/shard_map/dot_general | solution.py:432
  6.8 0.3 copy.11
  7.1 1.0 pad.11.clone
  8.1 53.1 %shard_map.66 = bf16[4,8,192,200]{3,2,1,0:T(8,128)(2,1)} custom-call(bf16[8,192,200]{2,1,0:T(8,128)(2,1)} %bitcast.32), custom_call_target="tpu_custom_call" | custom-call | tf_op jit(solution)/shard_map/pallas_call | solution.py:142
  61.2 3.7 %slice.16 = bf16[4,1504,200]{2,1,0:T(8,128)(2,1)} slice(bf16[4,1536,200]{2,1,0:T(8,128)(2,1)} %bitcast.29), slice={[0:4], [0:1504], [0:200]} | slice | bytes 4812800 | tf_op jit(solution)/shard_map/slice | solution.py:162
  64.9 12.9 %multiply_reduce_fusion = (f32[]{:T(128)}, bf16[200,1504]{1,0:T(8,128)(2,1)S(1)}) fusion(bf16[6016,200]{1,0:T(8,128)(2,1)} %bitcast.30, bf16[1,1504,6016]{2,1,0:T(8,128)(2,1)} %param.5), kind=kOutput, calls=%fused_computation.6 | convolution fusion | flops 3620428800 | bytes 21104132 | tf_op jit(solution)/shard_map/dot_general | solution.py:437
  77.9 2.1 convolution_bitcast_fusion.part
  80.0 12.9 %shard_map.67 = f32[200,200]{1,0:T(8,128)} custom-call(f32[1,200,200]{2,1,0:T(8,128)} %convolution_bitcast_fusion.part), custom_call_target="tpu_custom_call" | custom-call | tf_op jit(solution)/shard_map/pallas_call | solution.py:420
  92.9 1.6 multiply_reduce_fusion.1
  95.1 0.7 compare_select_fusion
  95.8 0.6 broadcast_select_fusion.stats
  96.4 1.3 convolution_convert_fusion.2
  97.7 0.9 pad.12.own
  98.6 0.3 copy.12
  98.9 1.0 pad.13.clone
  99.9 34.9 %shard_map.69 = bf16[1,8,192,200]{3,2,1,0:T(8,128)(2,1)} custom-call(bf16[8,192,200]{2,1,0:T(8,128)(2,1)} %bitcast.31), custom_call_target="tpu_custom_call" | custom-call | tf_op jit(solution)/shard_map/pallas_call | solution.py:142
  134.8 6.0 %convolution_convert_fusion = bf16[200,2500]{1,0:T(8,128)(2,1)S(1)} fusion(bf16[1504,2500]{0,1:T(8,128)(2,1)} %param.4, bf16[1,1536,200]{2,1,0:T(8,128)(2,1)} %bitcast.34), kind=kOutput, calls=%fused_computation.2 | convolution fusion | flops 1504499968 | bytes 9462336 | tf_op jit(solution)/shard_map/dot_general | solution.py:452
  140.8 1.3 reshape.35.part
  142.2 20.8 %shard_map.70 = f32[50,2500]{1,0:T(8,128)} custom-call(bf16[4,50,2500]{2,1,0:T(8,128)(2,1)} %reshape.35.part), custom_call_target="tpu_custom_call" | custom-call | tf_op jit(solution)/shard_map/pallas_call | solution.py:420
  163.0 89.1 %shard_map.68 = (f32[752,1504]{1,0:T(8,128)}, f32[8,128]{1,0:T(8,128)}) custom-call(bf16[200,1536]{1,0:T(8,128)(2,1)} %pad.12.own, f32[8,128]{1,0:T(8,128)} %broadcast_select_fusion.stats), custom_call_target="tpu_custom_call" | custom-call | tf_op jit(solution)/shard_map/pallas_call | solution.py:367
  252.1 1.3 fusion.9
  254.8 0.0 copy-start.1
  254.8 4.8 %copy.15 = f32[752,1504]{1,0:T(8,128)} copy(f32[752,1504]{1,0:T(8,128)} %get-tuple-element.16) | data formatting | bytes 9048064
  259.6 0.0 copy-done.1
  259.6 0.8 copy.16
  (1 shorter events, 0.0 us)
Async XLA Ops:
  0.6 1.2 copy-start
  254.8 4.8 %copy-start.1 = (f32[50,2500]{1,0:T(8,128)S(1)}, f32[50,2500]{1,0:T(8,128)}, u32[]{:S(2)}) copy-start(f32[50,2500]{1,0:T(8,128)} %shard_map.70) | copy-start | bytes 1500004
where the time goes:
time: 263 us
  Pallas kernels  211 us (80%)
  matrix products  27.3 us (10%)
  local copies, waits for them, and re-layouts  16.7 us (6%)
  between operations  4.95 us (2%)
  other arithmetic  2.84 us (1%)
    pallas_call x1, Pallas kernels, exchange_of(): pl.pallas_call(functools.partial(exchange_kernel, size_x, size_y, block),...  89.1 us
    pallas_call x2, Pallas kernels, reduce_gather(): pl.pallas_call(functools.partial(reduce_gather_kernel, size_x, size_y, wi...  88.1 us
    pallas_call x2, Pallas kernels, sum_over_y(): pl.pallas_call(functools.partial(sum_kernel, size_y, same), out_shape=jax...  33.7 us
    dot_general x1, matrix products, on_device(): lax.dot_general(admm, integrals[0], (((0,), (1,)), ((), ())), preferred_e...  12.9 us
    unnamed x8, local copies, waits for them, and re-layouts  7.39 us
    dot_general x1, matrix products, on_device(): lax.dot_general(applied_low, projector, (((0,), (0,)), ((), ())), preferr...  6 us

commit v1 on v0

v1 whole, which is shorter than its diff:
```python
import functools
import types

import jax
import jax.numpy as jnp
from jax import lax
from jax.experimental import pallas as pl
from jax.experimental.pallas import tpu as pltpu
from jax.sharding import PartitionSpec as P

MESH = pl.DeviceIdType.MESH
LIMIT = 63 * 1024 * 1024
LANE = 128
SUB = 2
F32, BF16 = jnp.float32, jnp.bfloat16


def factor(size):
    inner = 1
    while inner * inner * 4 <= size:
        inner *= 2
    return size // inner, inner


def up(value, unit):
    return -(-value // unit) * unit


def remote(src, dst, send, recv, dev):
    return pltpu.make_async_remote_copy(
        src_ref=src, dst_ref=dst, send_sem=send, recv_sem=recv, device_id=dev, device_id_type=MESH
    )


def dot(a, b, dims):
    return lax.dot_general(a, b, (dims, ((), ())), preferred_element_type=F32)


def layout(size_x, size_y, rows, depth, occ):
    g = types.SimpleNamespace(size_x=size_x, size_y=size_y, rows=rows, depth=depth, occ=occ)
    g.nz, g.nx = factor(size_x)
    g.ny = size_y // 2
    g.total = rows * size_y
    g.lz = up(-(-rows // g.nz), LANE)
    g.rx = up(-(-occ // g.nx), 8)
    g.off = [min(i * g.rx, occ - g.rx) for i in range(g.nx)]
    g.wide = up(rows, SUB * LANE)
    g.own = max(g.wide, g.nz * g.lz)
    g.units = g.wide // LANE
    g.subs = g.units // SUB
    g.na = g.subs - 1
    g.slots = g.na + g.nx
    g.block = g.total // size_x
    g.per = size_x // size_y
    g.window = max(up(i * g.block % LANE + g.block, LANE) for i in range(g.per))
    g.wu = g.window // LANE
    g.firsts = [min(i * g.block // LANE * LANE, g.wide - g.window) for i in range(g.per)]
    g.share = occ // size_y
    g.j = up(g.share, 8)
    g.step = 512
    g.chunks = -(-depth // g.step)
    g.group = 512 if g.wide % 512 == 0 else 256
    return g


def greet(size_x, size_y):
    gx, gy = lax.axis_index("gx"), lax.axis_index("gy")
    barrier = pltpu.get_barrier_semaphore()

    def hello(step, carry):
        other = lax.rem(gx * size_y + gy + step, size_x * size_y)
        pl.semaphore_signal(
            barrier, inc=1, device_id=(other // size_y, lax.rem(other, size_y)), device_id_type=MESH
        )
        return carry

    lax.fori_loop(1, size_x * size_y, hello, 0)
    pl.semaphore_wait(barrier, size_x * size_y - 1)


def whole_kernel(g, names, *refs):
    r = types.SimpleNamespace(**dict(zip(names, refs)))
    nz, nx, ny, occ, rows = g.nz, g.nx, g.ny, g.occ, g.rows
    gx, gy = lax.axis_index("gx"), lax.axis_index("gy")
    z, x = gx // nx, lax.rem(gx, nx)
    y, c = gy // 2, lax.rem(gy, 2)
    partner = (gx, gy + 1 - 2 * c)

    loads = [pltpu.make_async_copy(r.orb_h, r.orbv, r.load_sem.at[0])]
    for i in range(nz):
        low, high = i * g.lz, min((i + 1) * g.lz, rows)
        if high > low:
            loads.append(
                pltpu.make_async_copy(r.proj_h.at[low:high], r.projv.at[low:high], r.load_sem.at[i + 1])
            )
    for load in loads:
        load.start()
    span = SUB * LANE

    def int_load(s):
        low, high = s * span, min((s + 1) * span, rows)
        return pltpu.make_async_copy(r.int_h.at[0, low:high], r.integ.at[low:high], r.int_sem.at[s])

    for s in range(g.subs):
        int_load(s).start()
    greet(g.size_x, g.size_y)
    for load in loads:
        load.wait()

    def x_part(zz, e):
        to = lax.rem(x + e, nx)
        return remote(
            r.part.at[zz, to], r.xland.at[e, zz], r.send_p.at[zz, e], r.recv_p.at[zz, e], (z * nx + to, gy)
        )

    def project(i, carry):
        zz = lax.rem(z + 1 + i, nz)
        rows_of = r.projv[pl.ds(pl.multiple_of(zz * g.lz, LANE), g.lz), :]
        value = dot(r.orbv[...], rows_of, ((0,), (1,)))
        for xx in range(nx):
            r.part[zz, xx] = value[g.off[xx]:g.off[xx] + g.rx].astype(BF16)
        for e in range(1, nx):
            x_part(zz, e).start()
        return carry

    lax.fori_loop(0, nz, project, 0)

    def x_sum(zz):
        value = r.part[zz, x].astype(F32)
        for e in range(1, nx):
            x_part(zz, e).wait_recv()
            value = value + r.xland[e, zz].astype(F32)
        return value

    def z_part(d):
        to = lax.rem(z + d, nz)
        return remote(r.zsum.at[d], r.zland.at[d], r.send_q.at[d], r.recv_q.at[d], (to * nx + x, gy))

    for d in range(1, nz):
        r.zsum[d] = x_sum(lax.rem(z + d, nz)).astype(BF16)
        z_part(d).start()
    total = x_sum(z)
    for d in range(1, nz):
        z_part(d).wait_recv()
        total = total + r.zland[d].astype(F32)
    r.agb[gy, gx] = total.astype(BF16)

    def at(d, e):
        return lax.rem(z - d + nz, nz) * nx + lax.rem(x - e + nx, nx)

    def group(f, core):
        return lax.rem(y - f + ny, ny) * 2 + core

    def block_z(d, came):
        ref = r.agb.at[gy, at(d, 0) if came else gx]
        return remote(ref, ref, r.send_az.at[d], r.recv_az.at[d], (lax.rem(z + d, nz) * nx + x, gy))

    def block_x(gg, q, slot, e):
        ref = r.agb.at[gg, q]
        return remote(ref, ref, r.send_ax.at[slot, e], r.recv_ax.at[slot, e], (z * nx + lax.rem(x + e, nx), gy))

    def block_y(gg, q, slot, f):
        ref = r.agb.at[gg, q]
        return remote(ref, ref, r.send_ay.at[slot, f], r.recv_ay.at[slot, f], (gx, lax.rem(y + f, ny) * 2 + c))

    def block_c(d, e, f, core):
        ref = r.agb.at[group(f, core), at(d, e)]
        slot = (f * nz + d) * nx + e
        return remote(ref, ref, r.send_ac.at[slot], r.recv_ac.at[slot], partner)

    for d in range(1, nz):
        block_z(d, False).start()

    @pl.when(c == 0)
    def _():
        for d in range(nz):
            if d > 0:
                block_z(d, True).wait_recv()
            for e in range(1, nx):
                block_x(gy, at(d, 0), d, e).start()
            for f in range(1, ny):
                block_y(gy, at(d, 0), d * nx, f).start()
            block_c(d, 0, 0, c).start()
        for d in range(nz):
            for e in range(1, nx):
                block_x(gy, at(d, e), d, e).wait_recv()
                for f in range(1, ny):
                    block_y(gy, at(d, e), d * nx + e, f).start()
                block_c(d, e, 0, c).start()
        for d in range(nz):
            for e in range(nx):
                for f in range(1, ny):
                    block_y(group(f, c), at(d, e), d * nx + e, f).wait_recv()
                    block_c(d, e, f, c).start()

    @pl.when(c == 1)
    def _():
        for d in range(nz):
            if d > 0:
                block_z(d, True).wait_recv()
            for f in range(1, ny):
                block_y(gy, at(d, 0), d, f).start()
            for e in range(1, nx):
                block_x(gy, at(d, 0), d * ny, e).start()
            block_c(d, 0, 0, c).start()
        for d in range(nz):
            for f in range(1, ny):
                block_y(group(f, c), at(d, 0), d, f).wait_recv()
                for e in range(1, nx):
                    block_x(group(f, c), at(d, 0), d * ny + f, e).start()
                block_c(d, 0, f, c).start()
        for d in range(nz):
            for f in range(ny):
                for e in range(1, nx):
                    block_x(group(f, c), at(d, e), d * ny + f, e).wait_recv()
                    block_c(d, e, f, c).start()

    for d in range(nz):
        for e in range(nx):
            for f in range(ny):
                block_c(d, e, f, 1 - c).wait_recv()

    lane = lax.broadcasted_iota(jnp.int32, (g.rx, g.lz), 1)
    for gg in range(g.size_y):
        for zz in range(nz):
            width = min(g.lz, rows - zz * g.lz)
            if width <= 0:
                continue
            base = gg * rows + zz * g.lz
            for xx in range(nx):
                r.admm[g.off[xx]:g.off[xx] + g.rx, base:base + width] = r.agb[gg, zz * nx + xx][:, :width]
    for zz in range(nz):
        for xx in range(nx):
            piece = r.agb[gy, zz * nx + xx]
            piece = jnp.where(lane + zz * g.lz < rows, piece.astype(F32), 0.0).astype(BF16)
            r.own[g.off[xx]:g.off[xx] + g.rx, zz * g.lz:(zz + 1) * g.lz] = piece

    devices = g.size_x * g.size_y
    me = gx * g.size_y + gy
    root = gx // g.per
    root_y, root_c = root // 2, lax.rem(root, 2)
    turn = lax.rem(gx, g.per)
    first = 0
    for i in range(g.per):
        first = jnp.where(turn == i, g.firsts[i] // LANE, first)
    mine = gy == root
    below = (y != root_y) & (c == root_c)
    last = c != root_c

    def part_of(zz, slot):
        if slot < g.na:
            return r.cols.at[zz * nx + x, pl.ds(SUB * slot, SUB)]
        return r.cols.at[zz * nx + slot - g.na, pl.ds(SUB * g.na, SUB)]

    def upward(k, slot):
        ref = part_of(jnp.maximum(z - k, 0), slot)
        return remote(ref, ref, r.send_u.at[k, slot], r.recv_u.at[k, slot], (jnp.minimum(z + 1, nz - 1) * nx + x, gy))

    def downward(k, slot):
        ref = part_of(jnp.minimum(z + k, nz - 1), slot)
        return remote(ref, ref, r.send_d.at[k, slot], r.recv_d.at[k, slot], (jnp.maximum(z - 1, 0) * nx + x, gy))

    def sideways(zz, sub, e, came):
        ref = r.cols.at[zz * nx + (lax.rem(x - e + nx, nx) if came else x), pl.ds(SUB * sub, SUB)]
        return remote(
            ref, ref, r.send_x.at[zz, sub, e], r.recv_x.at[zz, sub, e], (z * nx + lax.rem(x + e, nx), gy)
        )

    def row_y(q, unit, f):
        spot = unit - first
        return remote(
            r.cols.at[q, unit], r.rows.at[q, spot], r.send_y.at[q, spot, f], r.recv_y.at[q], (gx, lax.rem(y + f, ny) * 2 + c)
        )

    def row_c(q, unit):
        spot = unit - first
        return remote(r.cols.at[q, unit], r.rows.at[q, spot], r.send_c.at[q, spot], r.recv_c.at[q], partner)

    def row_all(q):
        return remote(r.rows.at[q], r.rows.at[q], r.send_w.at[q], r.recv_c.at[q], partner)

    def row_came(q):
        return remote(r.rows.at[q], r.rows.at[q], r.send_w.at[q], r.recv_y.at[q], partner)

    def row_own(q):
        return pltpu.make_async_copy(r.cols.at[q, pl.ds(first, g.wu)], r.rows.at[q], r.row_sem.at[q])

    def pass_rows(q, sub):
        for h in range(SUB):
            unit = sub * SUB + h

            @pl.when(mine & (unit >= first) & (unit < first + g.wu))
            def _():
                for f in range(1, ny):
                    row_y(q, unit, f).start()
                row_c(q, unit).start()

    r.mixed[...] = jnp.zeros_like(r.mixed)
    r.trace[...] = jnp.zeros_like(r.trace)
    for s in range(g.subs):
        int_load(s).wait()
    spots = lax.broadcasted_iota(jnp.int32, (occ, span), 1)

    def half(i, carry):
        s = lax.rem(i + g.na, g.subs)
        start = pl.multiple_of(s * span, span)
        value = dot(r.admm[...], r.integ[pl.ds(start, span), :], ((1,), (1,)))
        value = jnp.where(spots + start < rows, value, 0.0)
        low = value.astype(BF16)
        for h in range(SUB):
            r.cols[gx, SUB * s + h] = low[:, h * LANE:(h + 1) * LANE]

        @pl.when(i == 0)
        def _():
            for e in range(1, nx):
                sideways(z, g.na, e, False).start()

        @pl.when(i > 0)
        def _():
            ref = r.cols.at[gx, pl.ds(SUB * s, SUB)]

            @pl.when(z < nz - 1)
            def _():
                remote(ref, ref, r.send_u.at[0, s], r.recv_u.at[0, s], (jnp.minimum(z + 1, nz - 1) * nx + x, gy)).start()

            @pl.when(z > 0)
            def _():
                remote(ref, ref, r.send_d.at[0, s], r.recv_d.at[0, s], (jnp.maximum(z - 1, 0) * nx + x, gy)).start()

            for e in range(1, nx):
                sideways(z, s, e, False).start()

        for h in range(SUB):
            unit = SUB * s + h

            @pl.when(mine & (unit >= first) & (unit < first + g.wu))
            def _():
                for f in range(1, ny):
                    row_y(gx, unit, f).start()
                row_c(gx, unit).start()

        exact = low.astype(F32)
        r.trace[...] += jnp.sum(exact * exact, axis=0, keepdims=True)
        r.mixed[...] += dot(r.own[:, pl.ds(start, span)], low, ((1,), (1,)))
        return carry

    lax.fori_loop(0, g.subs, half, 0)

    def z_send(k, slot):
        @pl.when((z >= k) & (z < nz - 1))
        def _():
            upward(k, slot).start()

        @pl.when((z + k < nz) & (z > 0))
        def _():
            downward(k, slot).start()

    for e in range(nx):
        for xx in range(nx):
            @pl.when(lax.rem(x - e + nx, nx) == xx)
            def _(e=e, xx=xx):
                if e > 0:
                    sideways(z, g.na, e, True).wait_recv()
                    pass_rows(z * nx + xx, g.na)
                z_send(0, g.na + xx)

    low = r.mixed[...].astype(BF16)
    row_i = lax.broadcasted_iota(jnp.int32, (g.j, occ), 0)
    col_i = lax.broadcasted_iota(jnp.int32, (g.j, occ), 1)
    for gg in range(g.size_y):
        pick = ((row_i < g.share) & (col_i == row_i + gg * g.share)).astype(F32).astype(BF16)
        r.mpart[gg] = dot(pick, low, ((1,), (0,))).astype(BF16)

    def mix_y(d):
        to = lax.rem(gy + d, g.size_y)
        return remote(r.mpart.at[to], r.mland.at[d], r.send_m.at[d], r.recv_m.at[d], (gx, to))

    for d in range(1, g.size_y):
        mix_y(d).start()
    total = r.mpart[gy].astype(F32)
    for d in range(1, g.size_y):
        mix_y(d).wait_recv()
        total = total + r.mland[d].astype(F32)
    r.mall[gy, gx] = total.astype(BF16)

    def mix_x(d, came):
        ref = r.mall.at[gy, lax.rem(gx - d + g.size_x, g.size_x) if came else gx]
        return remote(ref, ref, r.send_n.at[d], r.recv_n.at[d], (lax.rem(gx + d, g.size_x), gy))

    def mix_share(f, came):
        ref = r.mall.at[group(f, c) if came else gy]
        return remote(ref, ref, r.send_o.at[f], r.recv_o.at[f], (gx, lax.rem(y + f, ny) * 2 + c))

    def mix_core(f, core):
        ref = r.mall.at[group(f, core)]
        return remote(ref, ref, r.send_r.at[f], r.recv_r.at[f], partner)

    for d in range(1, g.size_x):
        mix_x(d, False).start()
    stat_lane = lax.broadcasted_iota(jnp.int32, (8, LANE), 1)
    energy_part, trace_part = jnp.sum(total * total), jnp.sum(r.trace[...])
    r.stats[...] = jnp.where(stat_lane == 0, energy_part, jnp.where(stat_lane == 1, trace_part, 0.0))

    def stat_copy(slot, step, to):
        return remote(
            r.stats, r.sland.at[slot], r.send_s.at[step], r.recv_s.at[slot], (to // g.size_y, lax.rem(to, g.size_y))
        )

    def tell(step, carry):
        stat_copy(me, step, lax.rem(me + step, devices)).start()
        return carry

    lax.fori_loop(1, devices, tell, 0)

    r.acc[...] = jnp.zeros_like(r.acc)
    r.applied[...] = jnp.zeros_like(r.applied)

    def units(ref, q, low, high):
        return jnp.concatenate([ref[q, u] for u in range(low, high)], axis=1)

    def exchange_term(q):
        @pl.when(mine)
        def _():
            row_own(q).wait()

        @pl.when(below)
        def _():
            row_came(q).wait_recv()
            row_all(q).start()

        @pl.when(last)
        def _():
            row_all(q).wait_recv()

        left = units(r.rows, q, 0, g.wu)
        for low in range(0, g.wide, g.group):
            right = units(r.cols, q, low // LANE, (low + g.group) // LANE)
            r.acc[:, low:low + g.group] += dot(left, right, ((0,), (0,)))

    def applied_term(q):
        right = units(r.cols, q, 0, g.units)
        for gg in range(g.size_y):
            r.applied[gg * g.j:(gg + 1) * g.j, :] += dot(r.mall[gg, q], right, ((1,), (0,)))

    def level(k, act):
        def one(i, carry):
            zz = z + jnp.where(i < nx, -k, k)

            @pl.when((zz >= 0) & (zz < nz))
            def _():
                act(zz * nx + lax.rem(x + lax.rem(i, nx), nx))

            return carry

        lax.fori_loop(0, 2 * nx if k else nx, one, 0)

    def arrive_x(k):
        for side in ((-1, 1) if k else (1,)):
            zz = z + side * k

            @pl.when((zz >= 0) & (zz < nz))
            def _(zz=zz):
                zz = jnp.clip(zz, 0, nz - 1)
                for sub in range(g.na):
                    for e in range(1, nx):
                        sideways(zz, sub, e, True).wait_recv()
                        pass_rows(zz * nx + lax.rem(x - e + nx, nx), sub)

        def own_rows(q):
            @pl.when(mine)
            def _():
                row_own(q).start()

        level(k, own_rows)

    def arrive_z(k, slot):
        for up_way in (True, False):
            zz = z - k if up_way else z + k

            @pl.when((zz >= 0) & (zz < nz))
            def _(zz=zz, up_way=up_way):
                zz = jnp.clip(zz, 0, nz - 1)
                sems = (r.send_u, r.recv_u) if up_way else (r.send_d, r.recv_d)
                ref = part_of(zz, slot)
                remote(ref, ref, sems[0].at[k - 1, slot], sems[1].at[k - 1, slot], partner).wait_recv()
                if k < nz - 1:
                    @pl.when((z < nz - 1) if up_way else (z > 0))
                    def _():
                        (upward if up_way else downward)(k, slot).start()
                if slot < g.na:
                    for e in range(1, nx):
                        sideways(zz, slot, e, False).start()
                    pass_rows(zz * nx + x, slot)
                else:
                    pass_rows(zz * nx + slot - g.na, g.na)

    for k in range(1, nz):
        for slot in range(g.slots):
            arrive_z(k, slot)
            if slot == min(2, g.slots - 1):
                arrive_x(k - 1)
            if slot == g.slots - 2:
                if k == 2:
                    for f in range(ny):
                        if f > 0:
                            mix_share(f, True).wait_recv()
                            mix_core(f, c).start()
                    for f in range(ny):
                        mix_core(f, 1 - c).wait_recv()
                    level(0, applied_term)
                level(k - 1, exchange_term)
                if k >= 2:
                    level(k - 1, applied_term)
        if k == 1:
            for d in range(1, g.size_x):
                mix_x(d, True).wait_recv()
            for f in range(1, ny):
                mix_share(f, False).start()
            mix_core(0, c).start()
    arrive_x(nz - 1)
    level(nz - 1, applied_term)

    low = r.applied[:, :rows].astype(BF16)

    def back_c(n, core):
        return remote(r.bpart.at[n, core], r.bland.at[n], r.send_v.at[n], r.recv_v.at[n], partner)

    def back_y(n, f):
        to = lax.rem(y + f, ny)
        return remote(r.bsum.at[n, to], r.byland.at[n, f], r.send_b.at[n, f], r.recv_b.at[n, f], (gx, to * 2 + c))

    for n in range(g.chunks):
        start, stop = n * g.step, min((n + 1) * g.step, g.depth)
        value = dot(low, r.projv[:rows, start:stop], ((1,), (0,)))
        for gg in range(g.size_y):
            r.bpart[n, gg % 2, gg // 2, :, :stop - start] = value[gg * g.j:(gg + 1) * g.j].astype(BF16)
        back_c(n, 1 - c).start()
    for n in range(g.chunks):
        back_c(n, 1 - c).wait_recv()
        total = r.bpart[n, c].astype(F32) + r.bland[n].astype(F32)
        r.bsum[n] = total.astype(BF16)
        for f in range(1, ny):
            back_y(n, f).start()
    level(nz - 1, exchange_term)
    for i in range(g.per):
        begin = i * g.block - g.firsts[i]

        @pl.when(turn == i)
        def _(begin=begin):
            r.exch[...] = r.acc[begin:begin + g.block, :rows]

    for n in range(g.chunks):
        total = r.bpart[n, c, y].astype(F32) + r.bland[n, y].astype(F32)
        for f in range(1, ny):
            back_y(n, f).wait_recv()
            total = total + r.byland[n, f].astype(F32)
        r.back[:, n * g.step:(n + 1) * g.step] = total

    def hear(step, carry):
        stat_copy(lax.rem(me + step, devices), step, me).wait_recv()
        return carry

    lax.fori_loop(1, devices, hear, 0)
    r.sland[me] = r.stats[...]
    r.sums[...] = jnp.sum(r.sland[...], axis=0)

    def told(step, carry):
        stat_copy(me, step, me).wait_send()
        return carry

    lax.fori_loop(1, devices, told, 0)
    for zz in range(nz):
        for e in range(1, nx):
            x_part(zz, e).wait_send()
    for d in range(1, nz):
        z_part(d).wait_send()
        block_z(d, False).wait_send()

    @pl.when(c == 0)
    def _():
        for d in range(nz):
            for e in range(1, nx):
                block_x(gy, at(d, 0), d, e).wait_send()
            for e in range(nx):
                for f in range(1, ny):
                    block_y(gy, at(d, e), d * nx + e, f).wait_send()

    @pl.when(c == 1)
    def _():
        for d in range(nz):
            for f in range(1, ny):
                block_y(gy, at(d, 0), d, f).wait_send()
            for f in range(ny):
                for e in range(1, nx):
                    block_x(group(f, c), at(d, 0), d * ny + f, e).wait_send()

    for d in range(nz):
        for e in range(nx):
            for f in range(ny):
                block_c(d, e, f, c).wait_send()
    for k in range(nz - 1):
        for slot in range(g.slots):
            @pl.when((z >= k) & (z < nz - 1))
            def _(k=k, slot=slot):
                upward(k, slot).wait_send()

            @pl.when((z + k < nz) & (z > 0))
            def _(k=k, slot=slot):
                downward(k, slot).wait_send()
    for e in range(1, nx):
        for zz in range(nz):
            for sub in range(g.na):
                sideways(zz, sub, e, False).wait_send()
        sideways(z, g.na, e, False).wait_send()

    def drain(q, carry):
        @pl.when(mine)
        def _():
            for spot in range(g.wu):
                for f in range(1, ny):
                    row_y(q, first + spot, f).wait_send()
                row_c(q, first + spot).wait_send()

        @pl.when(below)
        def _():
            row_all(q).wait_send()

        return carry

    lax.fori_loop(0, g.size_x, drain, 0)
    for d in range(1, g.size_y):
        mix_y(d).wait_send()
    for d in range(1, g.size_x):
        mix_x(d, False).wait_send()
    for f in range(1, ny):
        mix_share(f, False).wait_send()
    for f in range(ny):
        mix_core(f, c).wait_send()
    for n in range(g.chunks):
        back_c(n, 1 - c).wait_send()
        for f in range(1, ny):
            back_y(n, f).wait_send()


def whole(g, orbitals, projector, integrals):
    dma, vmem = pltpu.SemaphoreType.DMA, pltpu.VMEM
    nz, nx, ny, occ = g.nz, g.nx, g.ny, g.occ
    devices = g.size_x * g.size_y
    scratch = dict(
        orbv=vmem(orbitals.shape, BF16),
        projv=vmem((max(nz * g.lz, g.rows), g.depth), BF16),
        integ=vmem((g.wide, g.total), BF16),
        part=vmem((nz, nx, g.rx, g.lz), BF16),
        xland=vmem((nx, nz, g.rx, g.lz), BF16),
        zsum=vmem((nz, g.rx, g.lz), BF16),
        zland=vmem((nz, g.rx, g.lz), BF16),
        agb=vmem((g.size_y, g.size_x, g.rx, g.lz), BF16),
        admm=vmem((occ, g.total), BF16),
        own=vmem((occ, g.own), BF16),
        cols=vmem((g.size_x, g.units, occ, LANE), BF16),
        rows=vmem((g.size_x, g.wu, occ, LANE), BF16),
        acc=vmem((g.window, g.wide), F32),
        mixed=vmem((occ, occ), F32),
        trace=vmem((1, SUB * LANE), F32),
        mpart=vmem((g.size_y, g.j, occ), BF16),
        mland=vmem((g.size_y, g.j, occ), BF16),
        mall=vmem((g.size_y, g.size_x, g.j, occ), BF16),
        stats=vmem((8, LANE), F32),
        sland=vmem((devices, 8, LANE), F32),
        applied=vmem((g.size_y * g.j, g.wide), F32),
        bpart=vmem((g.chunks, 2, ny, g.j, g.step), BF16),
        bland=vmem((g.chunks, ny, g.j, g.step), BF16),
        bsum=vmem((g.chunks, ny, g.j, g.step), BF16),
        byland=vmem((g.chunks, ny, g.j, g.step), BF16),
        load_sem=dma((nz + 1,)),
        int_sem=dma((g.subs,)),
        row_sem=dma((g.size_x,)),
    )
    for letter, shape in dict(
        p=(nz, nx), q=(nz,), az=(nz,), ax=(nz * ny, nx), ay=(nz * nx, ny), ac=(nz * nx * ny,),
        u=(nz, g.slots), d=(nz, g.slots), x=(nz, g.subs, nx), m=(g.size_y,), n=(g.size_x,), o=(ny,), r=(ny,),
        s=(devices,), v=(g.chunks,), b=(g.chunks, ny),
    ).items():
        scratch["send_" + letter] = dma(shape)
        scratch["recv_" + letter] = dma(shape)
    scratch.update(
        send_y=dma((g.size_x, g.wu, ny)), recv_y=dma((g.size_x,)), send_c=dma((g.size_x, g.wu)),
        recv_c=dma((g.size_x,)), send_w=dma((g.size_x,)),
    )
    names = ["orb_h", "proj_h", "int_h", "exch", "back", "sums"] + list(scratch)
    return pl.pallas_call(
        functools.partial(whole_kernel, g, names),
        out_shape=(
            jax.ShapeDtypeStruct((g.block, g.rows), F32),
            jax.ShapeDtypeStruct((g.j, g.chunks * g.step), F32),
            jax.ShapeDtypeStruct((8, LANE), F32),
        ),
        in_specs=[pl.BlockSpec(memory_space=pl.ANY)] * 3,
        out_specs=[pl.BlockSpec(memory_space=pltpu.VMEM)] * 3,
        scratch_shapes=list(scratch.values()),
        compiler_params=pltpu.CompilerParams(collective_id=1, has_side_effects=True, vmem_limit_bytes=LIMIT),
    )(orbitals, projector, integrals)


def on_device(size_x, size_y, orbitals, projector, integrals):
    g = layout(size_x, size_y, projector.shape[0], projector.shape[1], orbitals.shape[1])
    exchange, back, sums = whole(g, orbitals, projector, integrals)
    energy_mean = -0.5 * sums[0, 0] / (g.total * g.occ)
    trace_mean = sums[0, 1] / g.total
    return (exchange, back[:g.share, :g.depth].T, energy_mean, trace_mean)


def solution(mesh):
    return jax.shard_map(
        functools.partial(on_device, mesh.shape["gx"], mesh.shape["gy"]),
        mesh=mesh,
        in_specs=(P("gx", None), P("gy", "gx"), P("gx", "gy", None)),
        out_specs=(P("gx", "gy"), P("gx", "gy"), P(), P()),
        check_vma=False,
    )
```

time: 263 us -> 146 us (0.56)
  the two profiles are of different devices: /device:TPU:7 before, /device:TPU:21 now
where the time goes in v1:
time: 146 us; the launch traced here: 145 us
  Pallas kernels  120 us (82%)
  local copies, waits for them, and re-layouts  21 us (14%)
  between operations  4.2 us (3%)
    pallas_call x1, Pallas kernels, whole(): pl.pallas_call(functools.partial(whole_kernel, g, names), out_shape=(jax....  120 us
    unnamed x3, local copies, waits for them, and re-layouts  17.7 us

profile of v1, /device:TPU:21, one launch (start us, length us, event | category | flops | bytes accessed | tf_op | source)
XLA Modules:
  0.0 145.2 jit_solution(13647612035747798985)
XLA Ops:
  0.6 2.4 %copy.7.refs_0_ = bf16[2500,200]{1,0:T(8,128)(2,1)} copy(bf16[2500,200]{0,1:T(8,128)(2,1)} %param.3) | data formatting | bytes 2000000 | tf_op args[0]
  3.0 10.6 %copy.8.refs_1_ = bf16[1504,2500]{1,0:T(8,128)(2,1)} copy(bf16[1504,2500]{0,1:T(8,128)(2,1)} %param.4) | data formatting | bytes 15040000 | tf_op args[1]
  13.6 120.0 %shard_map.66 = (f32[752,1504]{1,0:T(8,128)}, f32[56,2560]{1,0:T(8,128)}, f32[8,128]{1,0:T(8,128)}) custom-call(bf16[2500,200]{1,0:T(8,128)(2,1)} %copy.7.refs_0_, bf16[1504,2500]{1,0:T(8,128)(2,1)} %copy.8.refs_1_, bf16[1,1504,6016]{2,1,0:T(8,128)(2,1)} %refs_2_.1), custom_call_target="tpu_custom_call" | custom-call | tf_op jit(solution)/shard_map/pallas_call | solution.py:691
  133.6 1.3 fusion
  136.3 1.9 %slice_bitcast_fusion = f32[2500,50]{0,1:T(8,128)} fusion(f32[56,2560]{1,0:T(8,128)} %get-tuple-element.8), kind=kLoop, calls=%fused_computation | loop fusion | bytes 1000000 | tf_op jit(solution)/shard_map/transpose | solution.py:710
  138.2 4.8 %copy.10 = f32[752,1504]{1,0:T(8,128)} copy(f32[752,1504]{1,0:T(8,128)} %get-tuple-element.16) | data formatting | bytes 9048064

commit v2 on v1

--- a/solution.py
+++ b/solution.py
@@ -9,7 +9,7 @@
 from jax.sharding import PartitionSpec as P
 
 MESH = pl.DeviceIdType.MESH
-LIMIT = 63 * 1024 * 1024
+LIMIT = 57 * 1024 * 1024
 LANE = 128
 SUB = 2
 F32, BF16 = jnp.float32, jnp.bfloat16
@@ -63,6 +63,21 @@
     return g
 
 
+def flip(value, mask, size):
+    if size & (size - 1):
+        return lax.rem(value + mask, size)
+    bit = 1
+    while bit < size:
+        if mask & bit:
+            value = value + bit - 2 * bit * lax.rem(value // bit, 2)
+        bit *= 2
+    return value
+
+
+def unflip(value, mask, size):
+    return lax.rem(value - mask + size, size) if size & (size - 1) else flip(value, mask, size)
+
+
 def greet(size_x, size_y):
     gx, gy = lax.axis_index("gx"), lax.axis_index("gy")
     barrier = pltpu.get_barrier_semaphore()
@@ -87,12 +102,11 @@
     partner = (gx, gy + 1 - 2 * c)
 
     loads = [pltpu.make_async_copy(r.orb_h, r.orbv, r.load_sem.at[0])]
-    for i in range(nz):
-        low, high = i * g.lz, min((i + 1) * g.lz, rows)
-        if high > low:
-            loads.append(
-                pltpu.make_async_copy(r.proj_h.at[low:high], r.projv.at[low:high], r.load_sem.at[i + 1])
-            )
+    pieces = r.load_sem.shape[0] - 1
+    tall = up(-(-g.depth // pieces), 8)
+    for i in range(pieces):
+        low, high = i * tall, min((i + 1) * tall, g.depth)
+        loads.append(pltpu.make_async_copy(r.proj_h.at[low:high], r.projv.at[low:high], r.load_sem.at[i + 1]))
     for load in loads:
         load.start()
     span = SUB * LANE
@@ -101,11 +115,11 @@
         low, high = s * span, min((s + 1) * span, rows)
         return pltpu.make_async_copy(r.int_h.at[0, low:high], r.integ.at[low:high], r.int_sem.at[s])
 
-    for s in range(g.subs):
-        int_load(s).start()
     greet(g.size_x, g.size_y)
     for load in loads:
         load.wait()
+    for s in range(g.subs):
+        int_load(s).start()
 
     def x_part(zz, e):
         to = lax.rem(x + e, nx)
@@ -113,17 +127,25 @@
             r.part.at[zz, to], r.xland.at[e, zz], r.send_p.at[zz, e], r.recv_p.at[zz, e], (z * nx + to, gy)
         )
 
-    def project(i, carry):
-        zz = lax.rem(z + 1 + i, nz)
-        rows_of = r.projv[pl.ds(pl.multiple_of(zz * g.lz, LANE), g.lz), :]
-        value = dot(r.orbv[...], rows_of, ((0,), (1,)))
+    tail = (rows - 1) // g.lz
+
+    def put(zz, value):
         for xx in range(nx):
-            r.part[zz, xx] = value[g.off[xx]:g.off[xx] + g.rx].astype(BF16)
+            r.part[zz, xx, :, :value.shape[1]] = value[g.off[xx]:g.off[xx] + g.rx].astype(BF16)
+
+    for d in reversed(range(nz)):
+        zz = flip(z, d, nz)
+
+        @pl.when(zz < tail)
+        def _(zz=zz):
+            put(zz, dot(r.orbv[...], r.projv[:, pl.ds(pl.multiple_of(zz * g.lz, LANE), g.lz)], ((1,), (0,))))
+
+        @pl.when(zz == tail)
+        def _():
+            put(tail, dot(r.orbv[...], r.projv[:, tail * g.lz:rows], ((1,), (0,))))
+
         for e in range(1, nx):
             x_part(zz, e).start()
-        return carry
-
-    lax.fori_loop(0, nz, project, 0)
 
     def x_sum(zz):
         value = r.part[zz, x].astype(F32)
@@ -133,11 +155,10 @@
         return value
 
     def z_part(d):
-        to = lax.rem(z + d, nz)
-        return remote(r.zsum.at[d], r.zland.at[d], r.send_q.at[d], r.recv_q.at[d], (to * nx + x, gy))
-
-    for d in range(1, nz):
-        r.zsum[d] = x_sum(lax.rem(z + d, nz)).astype(BF16)
+        return remote(r.zsum.at[d], r.zland.at[d], r.send_q.at[d], r.recv_q.at[d], (flip(z, d, nz) * nx + x, gy))
+
+    for d in reversed(range(1, nz)):
+        r.zsum[d] = x_sum(flip(z, d, nz)).astype(BF16)
         z_part(d).start()
     total = x_sum(z)
     for d in range(1, nz):
@@ -146,14 +167,14 @@
     r.agb[gy, gx] = total.astype(BF16)
 
     def at(d, e):
-        return lax.rem(z - d + nz, nz) * nx + lax.rem(x - e + nx, nx)
+        return unflip(z, d, nz) * nx + lax.rem(x - e + nx, nx)
 
     def group(f, core):
         return lax.rem(y - f + ny, ny) * 2 + core
 
     def block_z(d, came):
         ref = r.agb.at[gy, at(d, 0) if came else gx]
-        return remote(ref, ref, r.send_az.at[d], r.recv_az.at[d], (lax.rem(z + d, nz) * nx + x, gy))
+        return remote(ref, ref, r.send_az.at[d], r.recv_az.at[d], (flip(z, d, nz) * nx + x, gy))
 
     def block_x(gg, q, slot, e):
         ref = r.agb.at[gg, q]
@@ -269,12 +290,18 @@
     def row_y(q, unit, f):
         spot = unit - first
         return remote(
-            r.cols.at[q, unit], r.rows.at[q, spot], r.send_y.at[q, spot, f], r.recv_y.at[q], (gx, lax.rem(y + f, ny) * 2 + c)
+            r.cols.at[q, unit], r.rows.at[q, spot], r.send_y.at[q, f], r.recv_y.at[q], (gx, lax.rem(y + f, ny) * 2 + c)
         )
 
     def row_c(q, unit):
         spot = unit - first
-        return remote(r.cols.at[q, unit], r.rows.at[q, spot], r.send_c.at[q, spot], r.recv_c.at[q], partner)
+        return remote(r.cols.at[q, unit], r.rows.at[q, spot], r.send_c.at[q], r.recv_c.at[q], partner)
+
+    def row_y_all(q, f):
+        return remote(r.rows.at[q], r.rows.at[q], r.send_y.at[q, f], r.recv_y.at[q], partner)
+
+    def row_c_all(q):
+        return remote(r.rows.at[q], r.rows.at[q], r.send_c.at[q], r.recv_c.at[q], partner)
 
     def row_all(q):
         return remote(r.rows.at[q], r.rows.at[q], r.send_w.at[q], r.recv_c.at[q], partner)
@@ -397,7 +424,7 @@
 
     for d in range(1, g.size_x):
         mix_x(d, False).start()
-    stat_lane = lax.broadcasted_iota(jnp.int32, (8, LANE), 1)
+    stat_lane = lax.broadcasted_iota(jnp.int32, (1, LANE), 1)
     energy_part, trace_part = jnp.sum(total * total), jnp.sum(r.trace[...])
     r.stats[...] = jnp.where(stat_lane == 0, energy_part, jnp.where(stat_lane == 1, trace_part, 0.0))
 
@@ -412,7 +439,7 @@
 
     lax.fori_loop(1, devices, tell, 0)
 
-    r.acc[...] = jnp.zeros_like(r.acc)
+    r.exch[...] = jnp.zeros_like(r.exch)
     r.applied[...] = jnp.zeros_like(r.applied)
 
     def units(ref, q, low, high):
@@ -433,9 +460,10 @@
             row_all(q).wait_recv()
 
         left = units(r.rows, q, 0, g.wu)
-        for low in range(0, g.wide, g.group):
-            right = units(r.cols, q, low // LANE, (low + g.group) // LANE)
-            r.acc[:, low:low + g.group] += dot(left, right, ((0,), (0,)))
+        for low in range(0, rows, g.group):
+            high = min(low + g.group, rows)
+            right = units(r.cols, q, low // LANE, up(high, LANE) // LANE)[:, :high - low]
+            r.exch[:, low:high] += dot(left, right, ((0,), (0,)))
 
     def applied_term(q):
         right = units(r.cols, q, 0, g.units)
@@ -494,9 +522,93 @@
                 else:
                     pass_rows(zz * nx + slot - g.na, g.na)
 
+    def drain_first():
+        for zz in range(nz):
+            for e in range(1, nx):
+                x_part(zz, e).wait_send()
+        for d in range(1, nz):
+            z_part(d).wait_send()
+            block_z(d, False).wait_send()
+
+        @pl.when(c == 0)
+        def _():
+            for d in range(nz):
+                for e in range(1, nx):
+                    block_x(gy, at(d, 0), d, e).wait_send()
+                for e in range(nx):
+                    for f in range(1, ny):
+                        block_y(gy, at(d, e), d * nx + e, f).wait_send()
+
+        @pl.when(c == 1)
+        def _():
+            for d in range(nz):
+                for f in range(1, ny):
+                    block_y(gy, at(d, 0), d, f).wait_send()
+                for f in range(ny):
+                    for e in range(1, nx):
+                        block_x(group(f, c), at(d, 0), d * ny + f, e).wait_send()
+
+        for d in range(nz):
+            for e in range(nx):
+                for f in range(ny):
+                    block_c(d, e, f, c).wait_send()
+
+    def drain_mixed():
+        for d in range(1, g.size_y):
+            mix_y(d).wait_send()
+        for d in range(1, g.size_x):
+            mix_x(d, False).wait_send()
+        for f in range(1, ny):
+            mix_share(f, False).wait_send()
+        for f in range(ny):
+            mix_core(f, c).wait_send()
+
+        def hear(step, carry):
+            stat_copy(lax.rem(me + step, devices), step, me).wait_recv()
+            return carry
+
+        lax.fori_loop(1, devices, hear, 0)
+
+        def told(step, carry):
+            stat_copy(me, step, me).wait_send()
+            return carry
+
+        lax.fori_loop(1, devices, told, 0)
+        r.sland[me] = r.stats[...]
+        r.sums[...] = jnp.sum(r.sland[...], axis=0)
+
+    def drain_level(k):
+        for slot in range(g.slots):
+            @pl.when((z >= k) & (z < nz - 1))
+            def _(slot=slot):
+                upward(k, slot).wait_send()
+
+            @pl.when((z + k < nz) & (z > 0))
+            def _(slot=slot):
+                downward(k, slot).wait_send()
+
+    def drain_x(k):
+        for e in range(1, nx):
+            for side in ((-1, 1) if k else (1,)):
+                zz = z + side * k
+
+                @pl.when((zz >= 0) & (zz < nz))
+                def _(zz=zz, e=e):
+                    zz = jnp.clip(zz, 0, nz - 1)
+                    for sub in range(g.na if k else g.na + 1):
+                        sideways(zz, sub, e, False).wait_send()
+
     for k in range(1, nz):
         for slot in range(g.slots):
             arrive_z(k, slot)
+            if slot == 1:
+                if k == 1:
+                    drain_first()
+                else:
+                    drain_level(k - 2)
+                    drain_x(k - 2)
+                if k == nz - 1:
+                    drain_mixed()
             if slot == min(2, g.slots - 1):
                 arrive_x(k - 1)
             if slot == g.slots - 2:
@@ -518,6 +630,7 @@
                 mix_share(f, False).start()
             mix_core(0, c).start()
     arrive_x(nz - 1)
+    drain_x(nz - 2)
     level(nz - 1, applied_term)
 
     low = r.applied[:, :rows].astype(BF16)
@@ -531,7 +644,7 @@
 
     for n in range(g.chunks):
         start, stop = n * g.step, min((n + 1) * g.step, g.depth)
-        value = dot(low, r.projv[:rows, start:stop], ((1,), (0,)))
+        value = dot(low, r.projv[start:stop, :], ((1,), (1,)))
         for gg in range(g.size_y):
             r.bpart[n, gg % 2, gg // 2, :, :stop - start] = value[gg * g.j:(gg + 1) * g.j].astype(BF16)
         back_c(n, 1 - c).start()
@@ -542,104 +655,35 @@
         for f in range(1, ny):
             back_y(n, f).start()
     level(nz - 1, exchange_term)
-    for i in range(g.per):
-        begin = i * g.block - g.firsts[i]
-
-        @pl.when(turn == i)
-        def _(begin=begin):
-            r.exch[...] = r.acc[begin:begin + g.block, :rows]
-
     for n in range(g.chunks):
         total = r.bpart[n, c, y].astype(F32) + r.bland[n, y].astype(F32)
         for f in range(1, ny):
             back_y(n, f).wait_recv()
             total = total + r.byland[n, f].astype(F32)
-        r.back[:, n * g.step:(n + 1) * g.step] = total
-
-    def hear(step, carry):
-        stat_copy(lax.rem(me + step, devices), step, me).wait_recv()
-        return carry
-
-    lax.fori_loop(1, devices, hear, 0)
-    r.sland[me] = r.stats[...]
-    r.sums[...] = jnp.sum(r.sland[...], axis=0)
-
-    def told(step, carry):
-        stat_copy(me, step, me).wait_send()
-        return carry
-
-    lax.fori_loop(1, devices, told, 0)
-    for zz in range(nz):
-        for e in range(1, nx):
-            x_part(zz, e).wait_send()
-    for d in range(1, nz):
-        z_part(d).wait_send()
-        block_z(d, False).wait_send()
-
-    @pl.when(c == 0)
-    def _():
-        for d in range(nz):
-            for e in range(1, nx):
-                block_x(gy, at(d, 0), d, e).wait_send()
-            for e in range(nx):
-                for f in range(1, ny):
-                    block_y(gy, at(d, e), d * nx + e, f).wait_send()
-
-    @pl.when(c == 1)
-    def _():
-        for d in range(nz):
-            for f in range(1, ny):
-                block_y(gy, at(d, 0), d, f).wait_send()
-            for f in range(ny):
-                for e in range(1, nx):
-                    block_x(group(f, c), at(d, 0), d * ny + f, e).wait_send()
-
-    for d in range(nz):
-        for e in range(nx):
-            for f in range(ny):
-                block_c(d, e, f, c).wait_send()
-    for k in range(nz - 1):
-        for slot in range(g.slots):
-            @pl.when((z >= k) & (z < nz - 1))
-            def _(k=k, slot=slot):
-                upward(k, slot).wait_send()
-
-            @pl.when((z + k < nz) & (z > 0))
-            def _(k=k, slot=slot):
-                downward(k, slot).wait_send()
-    for e in range(1, nx):
-        for zz in range(nz):
-            for sub in range(g.na):
-                sideways(zz, sub, e, False).wait_send()
-        sideways(z, g.na, e, False).wait_send()
-
-    def drain(q, carry):
-        @pl.when(mine)
-        def _():
-            for spot in range(g.wu):
-                for f in range(1, ny):
-                    row_y(q, first + spot, f).wait_send()
-                row_c(q, first + spot).wait_send()
-
-        @pl.when(below)
-        def _():
-            row_all(q).wait_send()
-
-        return carry
-
-    lax.fori_loop(0, g.size_x, drain, 0)
-    for d in range(1, g.size_y):
-        mix_y(d).wait_send()
-    for d in range(1, g.size_x):
-        mix_x(d, False).wait_send()
-    for f in range(1, ny):
-        mix_share(f, False).wait_send()
-    for f in range(ny):
-        mix_core(f, c).wait_send()
+        start, stop = n * g.step, min((n + 1) * g.step, g.depth)
+        r.back[:, start:stop] = total[:g.share, :stop - start]
+
+    drain_level(nz - 2)
+    drain_x(nz - 1)
     for n in range(g.chunks):
         back_c(n, 1 - c).wait_send()
         for f in range(1, ny):
             back_y(n, f).wait_send()
+
+    def drain(q, carry):
+        @pl.when(mine)
+        def _():
+            for f in range(1, ny):
+                row_y_all(q, f).wait_send()
+            row_c_all(q).wait_send()
+
+        @pl.when(below)
+        def _():
+            row_all(q).wait_send()
+
+        return carry
+
+    lax.fori_loop(0, g.size_x, drain, 0)
 
 
 def whole(g, orbitals, projector, integrals):
@@ -648,7 +692,7 @@
     devices = g.size_x * g.size_y
     scratch = dict(
         orbv=vmem(orbitals.shape, BF16),
-        projv=vmem((max(nz * g.lz, g.rows), g.depth), BF16),
+        projv=vmem(projector.shape, BF16),
         integ=vmem((g.wide, g.total), BF16),
         part=vmem((nz, nx, g.rx, g.lz), BF16),
         xland=vmem((nx, nz, g.rx, g.lz), BF16),
@@ -659,20 +703,19 @@
         own=vmem((occ, g.own), BF16),
         cols=vmem((g.size_x, g.units, occ, LANE), BF16),
         rows=vmem((g.size_x, g.wu, occ, LANE), BF16),
-        acc=vmem((g.window, g.wide), F32),
         mixed=vmem((occ, occ), F32),
         trace=vmem((1, SUB * LANE), F32),
         mpart=vmem((g.size_y, g.j, occ), BF16),
         mland=vmem((g.size_y, g.j, occ), BF16),
         mall=vmem((g.size_y, g.size_x, g.j, occ), BF16),
-        stats=vmem((8, LANE), F32),
-        sland=vmem((devices, 8, LANE), F32),
+        stats=vmem((1, LANE), F32),
+        sland=vmem((devices, 1, LANE), F32),
         applied=vmem((g.size_y * g.j, g.wide), F32),
         bpart=vmem((g.chunks, 2, ny, g.j, g.step), BF16),
         bland=vmem((g.chunks, ny, g.j, g.step), BF16),
         bsum=vmem((g.chunks, ny, g.j, g.step), BF16),
         byland=vmem((g.chunks, ny, g.j, g.step), BF16),
-        load_sem=dma((nz + 1,)),
+        load_sem=dma((5,)),
         int_sem=dma((g.subs,)),
         row_sem=dma((g.size_x,)),
     )
@@ -684,16 +727,16 @@
         scratch["send_" + letter] = dma(shape)
         scratch["recv_" + letter] = dma(shape)
     scratch.update(
-        send_y=dma((g.size_x, g.wu, ny)), recv_y=dma((g.size_x,)), send_c=dma((g.size_x, g.wu)),
+        send_y=dma((g.size_x, ny)), recv_y=dma((g.size_x,)), send_c=dma((g.size_x,)),
         recv_c=dma((g.size_x,)), send_w=dma((g.size_x,)),
     )
     names = ["orb_h", "proj_h", "int_h", "exch", "back", "sums"] + list(scratch)
     return pl.pallas_call(
         functools.partial(whole_kernel, g, names),
         out_shape=(
-            jax.ShapeDtypeStruct((g.block, g.rows), F32),
-            jax.ShapeDtypeStruct((g.j, g.chunks * g.step), F32),
-            jax.ShapeDtypeStruct((8, LANE), F32),
+            vmem((g.window, g.rows), F32),
+            vmem((g.share, g.depth), F32),
+            vmem((1, LANE), F32),
         ),
         in_specs=[pl.BlockSpec(memory_space=pl.ANY)] * 3,
         out_specs=[pl.BlockSpec(memory_space=pltpu.VMEM)] * 3,
@@ -702,12 +745,59 @@
     )(orbitals, projector, integrals)
 
 
+def finish_kernel(g, exch, back, sums, exch_o, back_o, energy, trace, sem, *spare):
+    tall = up(-(-g.block // 8), 8)
+    turn = lax.rem(lax.axis_index("gx"), g.per)
+    begins = [i * g.block - g.firsts[i] for i in range(g.per)]
+    skip, ready = 0, exch
+    if spare:
+        ready = spare[0]
+        for i in range(g.per):
+            @pl.when(turn == i)
+            def _(i=i):
+                ready[...] = exch[begins[i]:begins[i] + g.block, :]
+    else:
+        for i in range(g.per):
+            skip = jnp.where(turn == i, begins[i] // 8, skip)
+    copies = [pltpu.make_async_copy(back, back_o, sem.at[0])]
+    for i, low in enumerate(range(0, g.block, tall)):
+        high = min(low + tall, g.block)
+        source = ready.at[low:high] if spare else ready.at[pl.ds(pl.multiple_of(skip * 8 + low, 8), high - low)]
+        copies.append(pltpu.make_async_copy(source, exch_o.at[low:high], sem.at[i + 1]))
+    for copy in copies:
+        copy.start()
+    lane = lax.broadcasted_iota(jnp.int32, (1, LANE), 1)
+    value = sums[...]
+    energy[...] = jnp.sum(jnp.where(lane == 0, value, 0.0), keepdims=True) * (-0.5 / (g.total * g.occ))
+    trace[...] = jnp.sum(jnp.where(lane == 1, value, 0.0), keepdims=True) * (1.0 / g.total)
+    for copy in copies:
+        copy.wait()
+
+
+def finish(g, exch, back, sums):
+    vmem = pl.BlockSpec(memory_space=pltpu.VMEM)
+    hbm = pl.BlockSpec(memory_space=pl.ANY)
+    odd = any((i * g.block - g.firsts[i]) % 8 for i in range(g.per))
+    spare = [pltpu.VMEM((g.block, g.rows), F32)] if odd else []
+    return pl.pallas_call(
+        functools.partial(finish_kernel, g),
+        out_shape=(
+            jax.ShapeDtypeStruct((g.block, g.rows), F32),
+            jax.ShapeDtypeStruct(back.shape, F32),
+            jax.ShapeDtypeStruct((1, 1), F32),
+            jax.ShapeDtypeStruct((1, 1), F32),
+        ),
+        in_specs=[vmem] * 3,
+        out_specs=[hbm, hbm, vmem, vmem],
+        scratch_shapes=[pltpu.SemaphoreType.DMA((9,))] + spare,
+        compiler_params=pltpu.CompilerParams(vmem_limit_bytes=2 * 1024 * 1024 + 2 * (exch.size + back.size) * 4),
+    )(exch, back, sums)
+
+
 def on_device(size_x, size_y, orbitals, projector, integrals):
     g = layout(size_x, size_y, projector.shape[0], projector.shape[1], orbitals.shape[1])
-    exchange, back, sums = whole(g, orbitals, projector, integrals)
-    energy_mean = -0.5 * sums[0, 0] / (g.total * g.occ)
-    trace_mean = sums[0, 1] / g.total
-    return (exchange, back[:g.share, :g.depth].T, energy_mean, trace_mean)
+    exchange, back, energy, trace = finish(g, *whole(g, orbitals.T, projector.T, integrals))
+    return (exchange, back.T, energy.reshape(()), trace.reshape(()))
 
 
 def solution(mesh):

time: 146 us -> 113 us (0.77)
  local copies, waits for them, and re-layouts: 21 us -> 0 us
  Pallas kernels: 120 us -> 112 us
  between operations: 4.2 us -> 0.8 us
    unnamed x3 -> x0, local copies, waits for them, and re-layouts: 17.7 us -> none
    pallas_call x1 -> x2, Pallas kernels: 120 us -> 112 us  [the longest x1 109 us: whole(): pl.pallas_call(functools.partial(whole_kernel, g, names), out_shape=(vmem...]
    transpose x1 -> x0, local copies, waits for them, and re-layouts: 1.91 us -> none  [on_device(): return (exchange, back[:g.share, :g.depth].T, energy_mean, trace_mean)]
where the time goes in v2:
time: 113 us
  Pallas kernels  112 us (99%)
    pallas_call x1, Pallas kernels, whole(): pl.pallas_call(functools.partial(whole_kernel, g, names), out_shape=(vmem...  109 us
    pallas_call x1, Pallas kernels, finish(): pl.pallas_call(functools.partial(finish_kernel, g), out_shape=(jax.ShapeD...  2.92 us

profile of v2, /device:TPU:21, one launch (start us, length us, event | category | flops | bytes accessed | tf_op | source)
XLA Modules:
  0.0 112.9 jit_solution(7009109575267521481)
XLA Ops:
  0.6 109.2 %shard_map.66 = (f32[896,1504]{1,0:T(8,128)S(1)}, f32[50,2500]{1,0:T(8,128)S(1)}, f32[1,128]{1,0:T(1,128)S(1)}) custom-call(bf16[200,2500]{1,0:T(8,128)(2,1)} %bitcast.6, bf16[2500,1504]{1,0:T(8,128)(2,1)} %bitcast.5, bf16[1,1504,6016]{2,1,0:T(8,128)(2,1)} %refs_2_.1), custom_call_target="tpu_custom_call" | custom-call | tf_op jit(solution)/shard_map/pallas_call | solution.py:734
  109.9 2.9 %shard_map.67 = (f32[752,1504]{1,0:T(8,128)}, f32[50,2500]{1,0:T(8,128)}, f32[1,1]{1,0:T(1,128)}, f32[1,1]{1,0:T(1,128)}) custom-call(f32[896,1504]{1,0:T(8,128)S(1)} %get-tuple-element.11.exch, f32[50,2500]{1,0:T(8,128)S(1)} %get-tuple-element.12.back, f32[1,128]{1,0:T(1,128)S(1)} %get-tuple-element.13.sums), custom_call_target="tpu_custom_call" | custom-call | tf_op jit(solution)/shard_map/pallas_call | solution.py:782

commit v3 on v2

v3 whole, which is shorter than its diff:
```python
import functools
import types

import jax
import jax.numpy as jnp
from jax import lax
from jax.experimental import pallas as pl
from jax.experimental.pallas import tpu as pltpu
from jax.sharding import PartitionSpec as P

MESH = pl.DeviceIdType.MESH
LIMIT = 57 * 1024 * 1024
LANE = 128
SUB = 2
F32, BF16 = jnp.float32, jnp.bfloat16


def factor(size):
    inner = 1
    while inner * inner * 4 <= size:
        inner *= 2
    return size // inner, inner


def up(value, unit):
    return -(-value // unit) * unit


def remote(src, dst, send, recv, dev):
    return pltpu.make_async_remote_copy(
        src_ref=src, dst_ref=dst, send_sem=send, recv_sem=recv, device_id=dev, device_id_type=MESH
    )


def dot(a, b, dims):
    return lax.dot_general(a, b, (dims, ((), ())), preferred_element_type=F32)


def layout(size_x, size_y, rows, depth, occ):
    g = types.SimpleNamespace(size_x=size_x, size_y=size_y, rows=rows, depth=depth, occ=occ)
    g.nz, g.nx = factor(size_x)
    g.ny = size_y // 2
    g.total = rows * size_y
    g.lz = up(-(-rows // g.nz), LANE)
    g.waves = g.lz // LANE
    g.rx = up(-(-occ // g.nx), 8)
    g.off = [min(i * g.rx, occ - g.rx) for i in range(g.nx)]
    g.wide = up(rows, SUB * LANE)
    g.own = max(g.wide, g.nz * g.lz)
    g.units = g.wide // LANE
    g.subs = g.units // SUB
    g.na = g.subs - 1
    g.slots = g.na + g.nx
    g.block = g.total // size_x
    g.per = size_x // size_y
    g.window = max(up(i * g.block % LANE + g.block, LANE) for i in range(g.per))
    g.wu = g.window // LANE
    g.firsts = [min(i * g.block // LANE * LANE, g.wide - g.window) for i in range(g.per)]
    g.begins = [i * g.block - g.firsts[i] for i in range(g.per)]
    g.odd = any(begin % 8 for begin in g.begins)
    g.share = occ // size_y
    g.j = up(g.share, 8)
    g.step = 512
    g.chunks = -(-depth // g.step)
    g.group = 512 if g.wide % 512 == 0 else 256
    return g


def flip(value, mask, size):
    if size & (size - 1):
        return lax.rem(value + mask, size)
    bit = 1
    while bit < size:
        if mask & bit:
            value = value + bit - 2 * bit * lax.rem(value // bit, 2)
        bit *= 2
    return value


def unflip(value, mask, size):
    return lax.rem(value - mask + size, size) if size & (size - 1) else flip(value, mask, size)


def greet(size_x, size_y):
    gx, gy = lax.axis_index("gx"), lax.axis_index("gy")
    barrier = pltpu.get_barrier_semaphore()

    def hello(step, carry):
        other = lax.rem(gx * size_y + gy + step, size_x * size_y)
        pl.semaphore_signal(
            barrier, inc=1, device_id=(other // size_y, lax.rem(other, size_y)), device_id_type=MESH
        )
        return carry

    lax.fori_loop(1, size_x * size_y, hello, 0)
    pl.semaphore_wait(barrier, size_x * size_y - 1)


def whole_kernel(g, names, *refs):
    r = types.SimpleNamespace(**dict(zip(names, refs)))
    nz, nx, ny, occ, rows = g.nz, g.nx, g.ny, g.occ, g.rows
    gx, gy = lax.axis_index("gx"), lax.axis_index("gy")
    z, x = gx // nx, lax.rem(gx, nx)
    y, c = gy // 2, lax.rem(gy, 2)
    partner = (gx, gy + 1 - 2 * c)

    def left(ref, sem):
        remote(ref, ref, sem, r.spare, partner).wait_send()

    loads = [pltpu.make_async_copy(r.orb_h, r.orbv, r.load_sem.at[0])]
    pieces = r.load_sem.shape[0] - 1
    tall = up(-(-g.depth // pieces), 8)
    for i in range(pieces):
        low, high = i * tall, min((i + 1) * tall, g.depth)
        loads.append(pltpu.make_async_copy(r.proj_h.at[low:high], r.projv.at[low:high], r.load_sem.at[i + 1]))
    for load in loads:
        load.start()
    span = SUB * LANE

    def int_load(s):
        low, high = s * span, min((s + 1) * span, rows)
        return pltpu.make_async_copy(r.int_h.at[0, low:high], r.integ.at[low:high], r.int_sem.at[s])

    greet(g.size_x, g.size_y)
    for load in loads:
        load.wait()
    for s in range(g.subs):
        int_load(s).start()

    def x_part(zz, w, e):
        to = lax.rem(x + e, nx)
        return remote(
            r.part.at[zz, w, to], r.xland.at[e - 1, zz, w], r.send_p, r.recv_p.at[zz, w, e - 1], (z * nx + to, gy)
        )

    tail = (rows - 1) // g.lz

    def put(zz, value):
        for w in range(g.waves):
            seg = value[:, w * LANE:(w + 1) * LANE].astype(BF16)
            if seg.shape[1]:
                for xx in range(nx):
                    r.part[zz, w, xx, :, :seg.shape[1]] = seg[g.off[xx]:g.off[xx] + g.rx]

    for d in reversed(range(nz)):
        zz = flip(z, d, nz)

        @pl.when(zz < tail)
        def _(zz=zz):
            put(zz, dot(r.orbv[...], r.projv[:, pl.ds(pl.multiple_of(zz * g.lz, LANE), g.lz)], ((1,), (0,))))

        @pl.when(zz == tail)
        def _():
            put(tail, dot(r.orbv[...], r.projv[:, tail * g.lz:rows], ((1,), (0,))))

        for w in range(g.waves):
            for e in range(1, nx):
                x_part(zz, w, e).start()

    def x_sum(zz, w):
        value = r.part[zz, w, x].astype(F32)
        for e in range(1, nx):
            x_part(zz, w, e).wait_recv()
            value = value + r.xland[e - 1, zz, w].astype(F32)
        return value

    def z_part(d, w):
        return remote(
            r.zsum.at[d - 1, w], r.zland.at[d - 1, w], r.send_q, r.recv_q.at[d - 1, w], (flip(z, d, nz) * nx + x, gy)
        )

    for d in reversed(range(1, nz)):
        for w in range(g.waves):
            r.zsum[d - 1, w] = x_sum(flip(z, d, nz), w).astype(BF16)
            z_part(d, w).start()

    def at(d, e):
        return unflip(z, d, nz) * nx + lax.rem(x - e + nx, nx)

    def group(f, core):
        return lax.rem(y - f + ny, ny) * 2 + core

    def block_up(k, w):
        ref = r.agb.at[gy, w, jnp.maximum(z - k, 0) * nx + x]
        return remote(ref, ref, r.send_au.at[k], r.recv_au.at[k, w], (jnp.minimum(z + 1, nz - 1) * nx + x, gy))

    def block_down(k, w):
        ref = r.agb.at[gy, w, jnp.minimum(z + k, nz - 1) * nx + x]
        return remote(ref, ref, r.send_ad.at[k], r.recv_ad.at[k, w], (jnp.maximum(z - 1, 0) * nx + x, gy))

    def block_came(zz, k, w, rising):
        ref = r.agb.at[gy, w, zz * nx + x]
        sem = r.recv_au if rising else r.recv_ad
        return remote(ref, ref, r.spare, sem.at[k - 1, w], partner)

    def block_x(gg, w, q, slot, e):
        ref = r.agb.at[gg, w, q]
        return remote(
            ref, ref, r.send_ax, r.recv_ax.at[slot, w, e - 1], (z * nx + lax.rem(x + e, nx), gy)
        )

    def block_y(gg, w, q, slot, f):
        ref = r.agb.at[gg, w, q]
        return remote(
            ref, ref, r.send_ay, r.recv_ay.at[slot, w, f - 1], (gx, lax.rem(y + f, ny) * 2 + c)
        )

    def block_c(f, w, core):
        ref = r.agb.at[group(f, core), w]
        return remote(ref, ref, r.send_ac, r.recv_ac.at[f, w], partner)

    for w in range(g.waves):
        total = x_sum(z, w)
        for d in range(1, nz):
            z_part(d, w).wait_recv()
            total = total + r.zland[d - 1, w].astype(F32)
        r.agb[gy, w, gx] = total.astype(BF16)

        @pl.when(z < nz - 1)
        def _(w=w):
            block_up(0, w).start()

        @pl.when(z > 0)
        def _(w=w):
            block_down(0, w).start()

        for e in range(1, nx):
            block_x(gy, w, gx, jnp.where(c == 0, z, z * ny), e).start()
        for f in range(1, ny):
            block_y(gy, w, gx, jnp.where(c == 0, z * nx, z), f).start()

    def planes(k, act):
        for rising in ((True, False) if k else (True,)):
            zz = z - k if rising else z + k

            @pl.when((zz >= 0) & (zz < nz))
            def _(zz=zz, rising=rising):
                act(jnp.clip(zz, 0, nz - 1), rising)

    def first_stage(k, x_first):
        def act(zz, rising):
            for w in range(g.waves):
                block_came(zz, k, w, rising).wait_recv()
                if k < nz - 1:
                    @pl.when((z < nz - 1) if rising else (z > 0))
                    def _():
                        (block_up if rising else block_down)(k, w).start()
                for e in range(1, nx):
                    block_x(gy, w, zz * nx + x, zz if x_first else zz * ny, e).start()
                for f in range(1, ny):
                    block_y(gy, w, zz * nx + x, zz * nx if x_first else zz, f).start()

        planes(k, act)

    def second_stage(k, x_first):
        def act(zz, rising):
            for w in range(g.waves):
                if x_first:
                    for e in range(1, nx):
                        q = zz * nx + lax.rem(x - e + nx, nx)
                        block_x(gy, w, q, zz, e).wait_recv()
                        for f in range(1, ny):
                            block_y(gy, w, q, zz * nx + e, f).start()
                else:
                    for f in range(1, ny):
                        block_y(group(f, c), w, zz * nx + x, zz, f).wait_recv()
                        for e in range(1, nx):
                            block_x(group(f, c), w, zz * nx + x, zz * ny + f, e).start()

        planes(k, act)

    def third_stage(w, x_first):
        for f in range(1 if x_first else 0, ny):
            for d in range(nz):
                zz = flip(z, d, nz)
                if x_first:
                    for e in range(nx):
                        q = zz * nx + lax.rem(x - e + nx, nx)
                        block_y(group(f, c), w, q, zz * nx + e, f).wait_recv()
                else:
                    for e in range(1, nx):
                        q = zz * nx + lax.rem(x - e + nx, nx)
                        block_x(group(f, c), w, q, zz * ny + f, e).wait_recv()
            block_c(f, w, c).start()

    for x_first in (True, False):
        @pl.when(c == (0 if x_first else 1))
        def _(x_first=x_first):
            for k in range(1, nz):
                first_stage(k, x_first)
                second_stage(k - 1, x_first)
            second_stage(nz - 1, x_first)
            for w in range(g.waves):
                if x_first:
                    block_c(0, w, c).start()
                third_stage(w, x_first)

    for w in range(g.waves):
        for f in range(ny):
            block_c(f, w, 1 - c).wait_recv()

    lane = lax.broadcasted_iota(jnp.int32, (g.rx, g.lz), 1)

    def joined(gg, q):
        return jnp.concatenate([r.agb[gg, w, q] for w in range(g.waves)], axis=1)

    for gg in range(g.size_y):
        for zz in range(nz):
            width = min(g.lz, rows - zz * g.lz)
            if width <= 0:
                continue
            base = gg * rows + zz * g.lz
            for xx in range(nx):
                r.admm[g.off[xx]:g.off[xx] + g.rx, base:base + width] = joined(gg, zz * nx + xx)[:, :width]
    for zz in range(nz):
        for xx in range(nx):
            piece = joined(gy, zz * nx + xx)
            piece = jnp.where(lane + zz * g.lz < rows, piece.astype(F32), 0.0).astype(BF16)
            r.own[g.off[xx]:g.off[xx] + g.rx, zz * g.lz:(zz + 1) * g.lz] = piece

    devices = g.size_x * g.size_y
    me = gx * g.size_y + gy
    root = gx // g.per
    root_y, root_c = root // 2, lax.rem(root, 2)
    turn = lax.rem(gx, g.per)
    first = 0
    for i in range(g.per):
        first = jnp.where(turn == i, g.firsts[i] // LANE, first)
    mine = gy == root
    below = (y != root_y) & (c == root_c)
    last = c != root_c

    def part_of(zz, slot):
        if slot < g.na:
            return r.cols.at[zz * nx + x, pl.ds(SUB * slot, SUB)]
        return r.cols.at[zz * nx + slot - g.na, pl.ds(SUB * g.na, SUB)]

    def upward(k, slot):
        ref = part_of(jnp.maximum(z - k, 0), slot)
        return remote(ref, ref, r.send_u.at[k], r.recv_u.at[k, slot], (jnp.minimum(z + 1, nz - 1) * nx + x, gy))

    def downward(k, slot):
        ref = part_of(jnp.minimum(z + k, nz - 1), slot)
        return remote(ref, ref, r.send_d.at[k], r.recv_d.at[k, slot], (jnp.maximum(z - 1, 0) * nx + x, gy))

    def sideways(zz, sub, e, came):
        ref = r.cols.at[zz * nx + (lax.rem(x - e + nx, nx) if came else x), pl.ds(SUB * sub, SUB)]
        return remote(
            ref, ref, r.send_x.at[zz], r.recv_x.at[zz, sub, e - 1], (z * nx + lax.rem(x + e, nx), gy)
        )

    def row_y(q, unit, f):
        spot = unit - first
        return remote(
            r.cols.at[q, unit], r.rows.at[q, spot], r.send_y.at[f - 1], r.recv_y.at[q], (gx, lax.rem(y + f, ny) * 2 + c)
        )

    def row_c(q, unit):
        spot = unit - first
        return remote(r.cols.at[q, unit], r.rows.at[q, spot], r.send_c, r.recv_c.at[q], partner)

    def row_all(q):
        return remote(r.rows.at[q], r.rows.at[q], r.send_w, r.recv_c.at[q], partner)

    def row_came(q):
        return remote(r.rows.at[q], r.rows.at[q], r.spare, r.recv_y.at[q], partner)

    def row_own(q):
        return pltpu.make_async_copy(r.cols.at[q, pl.ds(first, g.wu)], r.rows.at[q], r.row_sem.at[q])

    def pass_rows(q, sub):
        for h in range(SUB):
            unit = sub * SUB + h

            @pl.when(mine & (unit >= first) & (unit < first + g.wu))
            def _():
                for f in range(1, ny):
                    row_y(q, unit, f).start()
                row_c(q, unit).start()

    r.mixed[...] = jnp.zeros_like(r.mixed)
    r.trace[...] = jnp.zeros_like(r.trace)
    for s in range(g.subs):
        int_load(s).wait()
    spots = lax.broadcasted_iota(jnp.int32, (occ, span), 1)

    def half(i, carry):
        s = lax.rem(i + g.na, g.subs)
        start = pl.multiple_of(s * span, span)
        value = dot(r.admm[...], r.integ[pl.ds(start, span), :], ((1,), (1,)))
        value = jnp.where(spots + start < rows, value, 0.0)
        low = value.astype(BF16)
        for h in range(SUB):
            r.cols[gx, SUB * s + h] = low[:, h * LANE:(h + 1) * LANE]

        @pl.when(i == 0)
        def _():
            for e in range(1, nx):
                sideways(z, g.na, e, False).start()

        @pl.when(i > 0)
        def _():
            ref = r.cols.at[gx, pl.ds(SUB * s, SUB)]

            @pl.when(z < nz - 1)
            def _():
                remote(ref, ref, r.send_u.at[0], r.recv_u.at[0, s], (jnp.minimum(z + 1, nz - 1) * nx + x, gy)).start()

            @pl.when(z > 0)
            def _():
                remote(ref, ref, r.send_d.at[0], r.recv_d.at[0, s], (jnp.maximum(z - 1, 0) * nx + x, gy)).start()

            for e in range(1, nx):
                sideways(z, s, e, False).start()

        for h in range(SUB):
            unit = SUB * s + h

            @pl.when(mine & (unit >= first) & (unit < first + g.wu))
            def _():
                for f in range(1, ny):
                    row_y(gx, unit, f).start()
                row_c(gx, unit).start()

        exact = low.astype(F32)
        r.trace[...] += jnp.sum(exact * exact, axis=0, keepdims=True)
        r.mixed[...] += dot(r.own[:, pl.ds(start, span)], low, ((1,), (1,)))
        return carry

    lax.fori_loop(0, g.subs, half, 0)

    def z_send(k, slot):
        @pl.when((z >= k) & (z < nz - 1))
        def _():
            upward(k, slot).start()

        @pl.when((z + k < nz) & (z > 0))
        def _():
            downward(k, slot).start()

    for e in range(nx):
        for xx in range(nx):
            @pl.when(lax.rem(x - e + nx, nx) == xx)
            def _(e=e, xx=xx):
                if e > 0:
                    sideways(z, g.na, e, True).wait_recv()
                    pass_rows(z * nx + xx, g.na)
                z_send(0, g.na + xx)

    low = r.mixed[...].astype(BF16)
    row_i = lax.broadcasted_iota(jnp.int32, (g.j, occ), 0)
    col_i = lax.broadcasted_iota(jnp.int32, (g.j, occ), 1)
    for gg in range(g.size_y):
        pick = ((row_i < g.share) & (col_i == row_i + gg * g.share)).astype(F32).astype(BF16)
        r.mpart[gg] = dot(pick, low, ((1,), (0,))).astype(BF16)

    def mix_y(d):
        to = lax.rem(gy + d, g.size_y)
        return remote(r.mpart.at[to], r.mland.at[d - 1], r.send_m, r.recv_m.at[d - 1], (gx, to))

    for d in range(1, g.size_y):
        mix_y(d).start()
    total = r.mpart[gy].astype(F32)
    for d in range(1, g.size_y):
        mix_y(d).wait_recv()
        total = total + r.mland[d - 1].astype(F32)
    r.mall[gy, gx] = total.astype(BF16)

    def mix_z(d, came):
        ref = r.mall.at[gy, at(d, 0) if came else gx]
        return remote(ref, ref, r.send_n, r.recv_n.at[d - 1], (flip(z, d, nz) * nx + x, gy))

    def mix_x(d, e, came):
        ref = r.mall.at[gy, at(d, e if came else 0)]
        return remote(ref, ref, r.send_k, r.recv_k.at[d, e - 1], (z * nx + lax.rem(x + e, nx), gy))

    def mix_share(f, came):
        ref = r.mall.at[group(f, c) if came else gy]
        return remote(ref, ref, r.send_o, r.recv_o.at[f - 1], (gx, lax.rem(y + f, ny) * 2 + c))

    def mix_core(f, core):
        ref = r.mall.at[group(f, core)]
        return remote(ref, ref, r.send_r, r.recv_r.at[f], partner)

    for d in range(1, nz):
        mix_z(d, False).start()
    for e in range(1, nx):
        mix_x(0, e, False).start()
    stat_lane = lax.broadcasted_iota(jnp.int32, (1, LANE), 1)
    energy_part, trace_part = jnp.sum(total * total), jnp.sum(r.trace[...])
    r.stats[...] = jnp.where(stat_lane == 0, energy_part, jnp.where(stat_lane == 1, trace_part, 0.0))

    def stat_copy(to):
        return remote(r.stats, r.sland.at[me], r.send_s, r.recv_s, (to // g.size_y, lax.rem(to, g.size_y)))

    def tell(step, carry):
        stat_copy(lax.rem(me + step, devices)).start()
        return carry

    lax.fori_loop(1, devices, tell, 0)

    r.acc[...] = jnp.zeros_like(r.acc)
    r.applied[...] = jnp.zeros_like(r.applied)

    def units(ref, q, low, high):
        return jnp.concatenate([ref[q, u] for u in range(low, high)], axis=1)

    def exchange_term(zz):
        for xx in range(nx):
            q = zz * nx + xx

            @pl.when(mine)
            def _(q=q):
                row_own(q).wait()

            @pl.when(below)
            def _(q=q):
                row_came(q).wait_recv()
                row_all(q).start()

        @pl.when(last)
        def _():
            for xx in range(nx):
                row_all(zz * nx + xx).wait_recv()

        lefts = [units(r.rows, zz * nx + xx, 0, g.wu) for xx in range(nx)]
        for low in range(0, rows, g.group):
            high = min(low + g.group, rows)
            value = r.acc[:, low:high]
            for xx in range(nx):
                right = units(r.cols, zz * nx + xx, low // LANE, up(high, LANE) // LANE)[:, :high - low]
                value = value + dot(lefts[xx], right, ((0,), (0,)))
            r.acc[:, low:high] = value

    def applied_term(zz):
        value = r.applied[...]
        for xx in range(nx):
            q = zz * nx + xx
            left = jnp.concatenate([r.mall[gg, q] for gg in range(g.size_y)], axis=0)
            value = value + dot(left, units(r.cols, q, 0, g.units), ((1,), (0,)))
        r.applied[...] = value

    def level(k, act):
        def one(i, carry):
            zz = z - k + 2 * k * i

            @pl.when((zz >= 0) & (zz < nz))
            def _():
                act(zz)

            return carry

        lax.fori_loop(0, 2 if k else 1, one, 0)

    def arrive_x(k):
        for side in ((-1, 1) if k else (1,)):
            zz = z + side * k

            @pl.when((zz >= 0) & (zz < nz))
            def _(zz=zz):
                zz = jnp.clip(zz, 0, nz - 1)
                for sub in range(g.na):
                    for e in range(1, nx):
                        sideways(zz, sub, e, True).wait_recv()
                        pass_rows(zz * nx + lax.rem(x - e + nx, nx), sub)

        def own_rows(zz):
            @pl.when(mine)
            def _():
                for xx in range(nx):
                    row_own(zz * nx + xx).start()

        level(k, own_rows)

    def arrive_z(k, slot):
        for up_way in (True, False):
            zz = z - k if up_way else z + k

            @pl.when((zz >= 0) & (zz < nz))
            def _(zz=zz, up_way=up_way):
                zz = jnp.clip(zz, 0, nz - 1)
                sem = r.recv_u if up_way else r.recv_d
                ref = part_of(zz, slot)
                remote(ref, ref, r.spare, sem.at[k - 1, slot], partner).wait_recv()
                if k < nz - 1:
                    @pl.when((z < nz - 1) if up_way else (z > 0))
                    def _():
                        (upward if up_way else downward)(k, slot).start()
                if slot < g.na:
                    for e in range(1, nx):
                        sideways(zz, slot, e, False).start()
                    pass_rows(zz * nx + x, slot)
                else:
                    pass_rows(zz * nx + slot - g.na, g.na)

    def drain_first():
        left(r.xland, r.send_p)
        left(r.zland, r.send_q)
        for k in range(nz - 1):
            @pl.when((z >= k) & (z < nz - 1))
            def _(k=k):
                left(r.agb.at[0, :, 0], r.send_au.at[k])

            @pl.when((z + k < nz) & (z > 0))
            def _(k=k):
                left(r.agb.at[0, :, 0], r.send_ad.at[k])

        left(r.agb.at[0:ny], r.send_ac)

        @pl.when(c == 0)
        def _():
            left(r.agb.at[0, :, 0:nz * (nx - 1)], r.send_ax)
            left(r.agb.at[0:ny - 1], r.send_ay)

        @pl.when(c == 1)
        def _():
            left(r.agb.at[0:ny * (nx - 1) // nx], r.send_ax)
            left(r.agb.at[0, :, 0:nz * (ny - 1)], r.send_ay)

    def drain_mixed():
        left(r.mland, r.send_m)
        left(r.mall.at[0, 0:nz - 1], r.send_n)
        left(r.mall.at[0, 0:nz * (nx - 1)], r.send_k)
        left(r.mall.at[0:ny - 1], r.send_o)
        left(r.mall.at[0:ny], r.send_r)
        others = r.sland.at[0:devices - 1]
        remote(others, others, r.send_s, r.recv_s, partner).wait()
        r.sland[me] = r.stats[...]
        r.sums[...] = jnp.sum(r.sland[...], axis=0)

    def drain_level(k):
        span_of = r.cols.at[0:SUB, 0:g.slots]

        @pl.when((z >= k) & (z < nz - 1))
        def _():
            left(span_of, r.send_u.at[k])

        @pl.when((z + k < nz) & (z > 0))
        def _():
            left(span_of, r.send_d.at[k])

    def drain_x(k):
        def act(zz, rising):
            left(r.cols.at[0:nx - 1, 0:SUB * (g.na if k else g.subs)], r.send_x.at[zz])

        planes(k, act)

    edge = (z == 0) | (z == nz - 1)

    def share_mixed():
        for d in range(nz):
            for e in range(1, nx):
                mix_x(d, e, True).wait_recv()
        for f in range(1, ny):
            mix_share(f, False).start()
        mix_core(0, c).start()

    def work(k):
        level(k - 1, exchange_term)
        if k == nz - 1:
            for f in range(ny):
                mix_core(f, 1 - c).wait_recv()
            for j in range(nz - 1):
                level(j, applied_term)

    for k in range(1, nz):
        for slot in range(g.slots):
            arrive_z(k, slot)
            if slot == 1:
                if k == 1:
                    drain_first()
                else:
                    drain_level(k - 2)
                    drain_x(k - 2)
            if slot == min(2, g.slots - 1):
                @pl.when(edge)
                def _(k=k):
                    arrive_x(k - 1)
            if slot == g.slots - 2:
                if k == 1:
                    for d in range(1, nz):
                        mix_z(d, True).wait_recv()
                        for e in range(1, nx):
                            mix_x(d, e, False).start()
                if k == nz - 1:
                    for f in range(1, ny):
                        mix_share(f, True).wait_recv()
                        mix_core(f, c).start()

                @pl.when(edge)
                def _(k=k):
                    work(k)

        @pl.when(jnp.logical_not(edge))
        def _(k=k):
            arrive_x(k - 1)
            if k == nz - 2:
                share_mixed()
            work(k)

        if k == nz - 2:
            @pl.when(edge)
            def _():
                share_mixed()
    drain_mixed()
    arrive_x(nz - 1)
    drain_x(nz - 2)
    level(nz - 1, applied_term)

    low = r.applied[:, :rows].astype(BF16)

    def back_c(n, core):
        return remote(r.bpart.at[n, core], r.bland.at[n], r.send_v, r.recv_v.at[n], partner)

    def back_y(n, f):
        to = lax.rem(y + f, ny)
        return remote(r.bsum.at[n, to], r.byland.at[n, f - 1], r.send_b, r.recv_b.at[n, f - 1], (gx, to * 2 + c))

    def back_on(n):
        back_c(n, 1 - c).wait_recv()
        total = r.bpart[n, c].astype(F32) + r.bland[n].astype(F32)
        r.bsum[n] = total.astype(BF16)
        for f in range(1, ny):
            back_y(n, f).start()

    for n in range(g.chunks):
        start, stop = n * g.step, min((n + 1) * g.step, g.depth)
        value = dot(low, r.projv[start:stop, :], ((1,), (1,)))
        for gg in range(g.size_y):
            r.bpart[n, gg % 2, gg // 2, :, :stop - start] = value[gg * g.j:(gg + 1) * g.j].astype(BF16)
        back_c(n, 1 - c).start()
        if n > 0:
            back_on(n - 1)
    back_on(g.chunks - 1)
    level(nz - 1, exchange_term)
    if g.odd:
        result = pltpu.make_async_copy(r.acc, r.exch, r.out_sem)
    else:
        skip = 0
        for i in range(g.per):
            skip = jnp.where(turn == i, g.begins[i] // 8, skip)
        result = pltpu.make_async_copy(
            r.acc.at[pl.ds(pl.multiple_of(skip * 8, 8), g.block)], r.exch, r.out_sem
        )
    result.start()
    for n in range(g.chunks):
        total = r.bpart[n, c, y].astype(F32) + r.bland[n, y].astype(F32)
        for f in range(1, ny):
            back_y(n, f).wait_recv()
            total = total + r.byland[n, f - 1].astype(F32)
        start, stop = n * g.step, min((n + 1) * g.step, g.depth)
        r.back[:, start:stop] = total[:g.share, :stop - start]

    drain_level(nz - 2)
    drain_x(nz - 1)
    left(r.bland, r.send_v)
    left(r.byland, r.send_b)

    @pl.when(mine)
    def _():
        for f in range(1, ny):
            left(r.rows, r.send_y.at[f - 1])
        left(r.rows, r.send_c)

    @pl.when(below)
    def _():
        left(r.rows, r.send_w)

    result.wait()


def whole(g, orbitals, projector, integrals):
    dma, vmem = pltpu.SemaphoreType.DMA, pltpu.VMEM
    nz, nx, ny, occ = g.nz, g.nx, g.ny, g.occ
    devices = g.size_x * g.size_y
    scratch = dict(
        orbv=vmem(orbitals.shape, BF16),
        projv=vmem(projector.shape, BF16),
        integ=vmem((g.wide, g.total), BF16),
        part=vmem((nz, g.waves, nx, g.rx, LANE), BF16),
        xland=vmem((nx - 1, nz, g.waves, g.rx, LANE), BF16),
        zsum=vmem((nz - 1, g.waves, g.rx, LANE), BF16),
        zland=vmem((nz - 1, g.waves, g.rx, LANE), BF16),
        agb=vmem((g.size_y, g.waves, g.size_x, g.rx, LANE), BF16),
        admm=vmem((occ, g.total), BF16),
        own=vmem((occ, g.own), BF16),
        cols=vmem((g.size_x, g.units, occ, LANE), BF16),
        rows=vmem((g.size_x, g.wu, occ, LANE), BF16),
        acc=vmem((g.window, g.rows), F32),
        mixed=vmem((occ, occ), F32),
        out_sem=dma(()),
        trace=vmem((1, SUB * LANE), F32),
        mpart=vmem((g.size_y, g.j, occ), BF16),
        mland=vmem((g.size_y - 1, g.j, occ), BF16),
        mall=vmem((g.size_y, g.size_x, g.j, occ), BF16),
        stats=vmem((1, LANE), F32),
        sland=vmem((devices, 1, LANE), F32),
        applied=vmem((g.size_y * g.j, g.wide), F32),
        bpart=vmem((g.chunks, 2, ny, g.j, g.step), BF16),
        bland=vmem((g.chunks, ny, g.j, g.step), BF16),
        bsum=vmem((g.chunks, ny, g.j, g.step), BF16),
        byland=vmem((g.chunks, ny - 1, g.j, g.step), BF16),
        load_sem=dma((5,)),
        int_sem=dma((g.subs,)),
        row_sem=dma((g.size_x,)),
    )
    one = ()
    for letter, sends, arrivals in (
        ("p", one, (nz, g.waves, nx - 1)),
        ("q", one, (nz - 1, g.waves)),
        ("au", (nz - 1,), (nz - 1, g.waves)),
        ("ad", (nz - 1,), (nz - 1, g.waves)),
        ("ax", one, (nz * ny, g.waves, nx - 1)),
        ("ay", one, (nz * nx, g.waves, ny - 1)),
        ("ac", one, (ny, g.waves)),
        ("u", (nz - 1,), (nz - 1, g.slots)),
        ("d", (nz - 1,), (nz - 1, g.slots)),
        ("x", (nz,), (nz, g.subs, nx - 1)),
        ("m", one, (g.size_y - 1,)),
        ("n", one, (nz - 1,)),
        ("k", one, (nz, nx - 1)),
        ("o", one, (ny - 1,)),
        ("r", one, (ny,)),
        ("s", one, one),
        ("v", one, (g.chunks,)),
        ("b", one, (g.chunks, ny - 1)),
        ("y", (ny - 1,), (g.size_x,)),
        ("c", one, (g.size_x,)),
    ):
        scratch["send_" + letter] = dma(sends)
        scratch["recv_" + letter] = dma(arrivals)
    scratch.update(send_w=dma(one), spare=dma(one))
    names = ["orb_h", "proj_h", "int_h", "exch", "back", "sums"] + list(scratch)
    return pl.pallas_call(
        functools.partial(whole_kernel, g, names),
        out_shape=(
            vmem((g.window if g.odd else g.block, g.rows), F32),
            vmem((g.share, g.depth), F32),
            vmem((1, LANE), F32),
        ),
        in_specs=[pl.BlockSpec(memory_space=pl.ANY)] * 3,
        out_specs=[pl.BlockSpec(memory_space=pl.ANY)] + [pl.BlockSpec(memory_space=pltpu.VMEM)] * 2,
        scratch_shapes=list(scratch.values()),
        compiler_params=pltpu.CompilerParams(collective_id=1, has_side_effects=True, vmem_limit_bytes=LIMIT),
    )(orbitals, projector, integrals)


def finish_kernel(g, exch, back, sums, exch_o, back_o, energy, trace, sem, *spare):
    tall = up(-(-g.block // 8), 8)
    ready = exch
    if spare:
        ready = spare[0]
        turn = lax.rem(lax.axis_index("gx"), g.per)
        for i in range(g.per):
            @pl.when(turn == i)
            def _(i=i):
                ready[...] = exch[g.begins[i]:g.begins[i] + g.block, :]
    copies = [pltpu.make_async_copy(back, back_o, sem.at[0])]
    for i, low in enumerate(range(0, g.block, tall)):
        high = min(low + tall, g.block)
        copies.append(pltpu.make_async_copy(ready.at[low:high], exch_o.at[low:high], sem.at[i + 1]))
    for copy in copies:
        copy.start()
    lane = lax.broadcasted_iota(jnp.int32, (1, LANE), 1)
    value = sums[...]
    energy[...] = jnp.sum(jnp.where(lane == 0, value, 0.0), keepdims=True) * (-0.5 / (g.total * g.occ))
    trace[...] = jnp.sum(jnp.where(lane == 1, value, 0.0), keepdims=True) * (1.0 / g.total)
    for copy in copies:
        copy.wait()


def finish(g, exch, back, sums):
    vmem = pl.BlockSpec(memory_space=pltpu.VMEM)
    hbm = pl.BlockSpec(memory_space=pl.ANY)
    spare = [pltpu.VMEM((g.block, g.rows), F32)] if g.odd else []
    return pl.pallas_call(
        functools.partial(finish_kernel, g),
        out_shape=(
            jax.ShapeDtypeStruct((g.block, g.rows), F32),
            jax.ShapeDtypeStruct(back.shape, F32),
            jax.ShapeDtypeStruct((1, 1), F32),
            jax.ShapeDtypeStruct((1, 1), F32),
        ),
        in_specs=[vmem] * 3,
        out_specs=[hbm, hbm, vmem, vmem],
        scratch_shapes=[pltpu.SemaphoreType.DMA((9,))] + spare,
        compiler_params=pltpu.CompilerParams(vmem_limit_bytes=2 * 1024 * 1024 + 2 * (exch.size + back.size) * 4),
    )(exch, back, sums)


def on_device(size_x, size_y, orbitals, projector, integrals):
    g = layout(size_x, size_y, projector.shape[0], projector.shape[1], orbitals.shape[1])
    exchange, back, energy, trace = finish(g, *whole(g, orbitals.T, projector.T, integrals))
    return (exchange, back.T, energy.reshape(()), trace.reshape(()))


def solution(mesh):
    return jax.shard_map(
        functools.partial(on_device, mesh.shape["gx"], mesh.shape["gy"]),
        mesh=mesh,
        in_specs=(P("gx", None), P("gy", "gx"), P("gx", "gy", None)),
        out_specs=(P("gx", "gy"), P("gx", "gy"), P(), P()),
        check_vma=False,
    )
```

time: 113 us -> 109 us (0.965); the launches traced: 113 us -> 108 us
  Pallas kernels: 112 us -> 107 us
    pallas_call x1, Pallas kernels: 109 us -> 104 us  [whole(): pl.pallas_call(functools.partial(whole_kernel, g, names), out_shape=(vmem...]
where the time goes in v3:
time: 109 us; the launch traced here: 108 us
  Pallas kernels  107 us (98%)
    pallas_call x1, Pallas kernels, whole(): pl.pallas_call(functools.partial(whole_kernel, g, names), out_shape=(vmem...  104 us
    pallas_call x1, Pallas kernels, finish(): pl.pallas_call(functools.partial(finish_kernel, g), out_shape=(jax.ShapeD...  2.92 us

profile of v3, /device:TPU:21, one launch (start us, length us, event | category | flops | bytes accessed | tf_op | source)
XLA Modules:
  0.0 107.5 jit_solution(2739264858669449262)
XLA Ops:
  0.6 103.8 %shard_map.66 = (f32[752,1504]{1,0:T(8,128)S(1)}, f32[50,2500]{1,0:T(8,128)S(1)}, f32[1,128]{1,0:T(1,128)S(1)}) custom-call(bf16[200,2500]{1,0:T(8,128)(2,1)} %bitcast.6, bf16[2500,1504]{1,0:T(8,128)(2,1)} %bitcast.5, bf16[1,1504,6016]{2,1,0:T(8,128)(2,1)} %refs_2_.1), custom_call_target="tpu_custom_call" | custom-call | tf_op jit(solution)/shard_map/pallas_call | solution.py:834
  104.4 2.9 %shard_map.67 = (f32[752,1504]{1,0:T(8,128)}, f32[50,2500]{1,0:T(8,128)}, f32[1,1]{1,0:T(1,128)}, f32[1,1]{1,0:T(1,128)}) custom-call(f32[752,1504]{1,0:T(8,128)S(1)} %get-tuple-element.11.exch, f32[50,2500]{1,0:T(8,128)S(1)} %get-tuple-element.12.back, f32[1,128]{1,0:T(1,128)S(1)} %get-tuple-element.13.sums), custom_call_target="tpu_custom_call" | custom-call | tf_op jit(solution)/shard_map/pallas_call | solution.py:876

commit v4 on v3

--- a/solution.py
+++ b/solution.py
@@ -205,9 +205,9 @@
             ref, ref, r.send_ay, r.recv_ay.at[slot, w, f - 1], (gx, lax.rem(y + f, ny) * 2 + c)
         )
 
-    def block_c(f, w, core):
-        ref = r.agb.at[group(f, core), w]
-        return remote(ref, ref, r.send_ac, r.recv_ac.at[f, w], partner)
+    def block_c(f, zz, core):
+        ref = r.agb.at[group(f, core), :, pl.ds(zz * nx, nx)]
+        return remote(ref, ref, r.send_ac, r.recv_ac.at[f, zz], partner)
 
     for w in range(g.waves):
         total = x_sum(z, w)
@@ -269,19 +269,23 @@
 
         planes(k, act)
 
-    def third_stage(w, x_first):
-        for f in range(1 if x_first else 0, ny):
-            for d in range(nz):
-                zz = flip(z, d, nz)
-                if x_first:
-                    for e in range(nx):
-                        q = zz * nx + lax.rem(x - e + nx, nx)
-                        block_y(group(f, c), w, q, zz * nx + e, f).wait_recv()
-                else:
-                    for e in range(1, nx):
-                        q = zz * nx + lax.rem(x - e + nx, nx)
-                        block_x(group(f, c), w, q, zz * ny + f, e).wait_recv()
-            block_c(f, w, c).start()
+    def third_stage(k, x_first):
+        def act(zz, rising):
+            if x_first:
+                block_c(0, zz, c).start()
+            for f in range(1 if x_first else 0, ny):
+                for w in range(g.waves):
+                    if x_first:
+                        for e in range(nx):
+                            q = zz * nx + lax.rem(x - e + nx, nx)
+                            block_y(group(f, c), w, q, zz * nx + e, f).wait_recv()
+                    else:
+                        for e in range(1, nx):
+                            q = zz * nx + lax.rem(x - e + nx, nx)
+                            block_x(group(f, c), w, q, zz * ny + f, e).wait_recv()
+                block_c(f, zz, c).start()
+
+        planes(k, act)
 
     for x_first in (True, False):
         @pl.when(c == (0 if x_first else 1))
@@ -289,15 +293,15 @@
             for k in range(1, nz):
                 first_stage(k, x_first)
                 second_stage(k - 1, x_first)
+                if k > 1:
+                    third_stage(k - 2, x_first)
             second_stage(nz - 1, x_first)
-            for w in range(g.waves):
-                if x_first:
-                    block_c(0, w, c).start()
-                third_stage(w, x_first)
-
-    for w in range(g.waves):
-        for f in range(ny):
-            block_c(f, w, 1 - c).wait_recv()
+            third_stage(nz - 2, x_first)
+            third_stage(nz - 1, x_first)
+
+    for f in range(ny):
+        for zz in range(nz):
+            block_c(f, zz, 1 - c).wait_recv()
 
     lane = lax.broadcasted_iota(jnp.int32, (g.rx, g.lz), 1)
 
@@ -656,12 +660,17 @@
         mix_core(0, c).start()
 
     def work(k):
-        level(k - 1, exchange_term)
-        if k == nz - 1:
+        if k < nz - 1:
+            level(k - 1, exchange_term)
+        else:
             for f in range(ny):
                 mix_core(f, 1 - c).wait_recv()
-            for j in range(nz - 1):
+            for j in range(nz - 2):
                 level(j, applied_term)
+
+            @pl.when(edge)
+            def _():
+                level(nz - 2, applied_term)
 
     for k in range(1, nz):
         for slot in range(g.slots):
@@ -693,10 +702,15 @@
 
         @pl.when(jnp.logical_not(edge))
         def _(k=k):
+            if k == nz - 1:
+                work(k)
             arrive_x(k - 1)
             if k == nz - 2:
                 share_mixed()
-            work(k)
+            if k < nz - 1:
+                work(k)
+            else:
+                level(nz - 2, applied_term)
 
         if k == nz - 2:
             @pl.when(edge)
@@ -732,6 +746,7 @@
         if n > 0:
             back_on(n - 1)
     back_on(g.chunks - 1)
+    level(nz - 2, exchange_term)
     level(nz - 1, exchange_term)
     if g.odd:
         result = pltpu.make_async_copy(r.acc, r.exch, r.out_sem)
@@ -812,7 +827,7 @@
         ("ad", (nz - 1,), (nz - 1, g.waves)),
         ("ax", one, (nz * ny, g.waves, nx - 1)),
         ("ay", one, (nz * nx, g.waves, ny - 1)),
-        ("ac", one, (ny, g.waves)),
+        ("ac", one, (ny, nz)),
         ("u", (nz - 1,), (nz - 1, g.slots)),
         ("d", (nz - 1,), (nz - 1, g.slots)),
         ("x", (nz,), (nz, g.subs, nx - 1)),

time: 109 us -> 105 us (0.963)
  Pallas kernels: 107 us -> 103 us
    pallas_call x1, Pallas kernels: 104 us -> 100 us  [whole(): pl.pallas_call(functools.partial(whole_kernel, g, names), out_shape=(vmem...]
where the time goes in v4:
time: 105 us; the launch traced here: 104 us
  Pallas kernels  103 us (98%)
    pallas_call x1, Pallas kernels, whole(): pl.pallas_call(functools.partial(whole_kernel, g, names), out_shape=(vmem...  100 us
    pallas_call x1, Pallas kernels, finish(): pl.pallas_call(functools.partial(finish_kernel, g), out_shape=(jax.ShapeD...  2.92 us

profile of v4, /device:TPU:21, one launch (start us, length us, event | category | flops | bytes accessed | tf_op | source)
XLA Modules:
  0.0 104.1 jit_solution(5342789985484658106)
XLA Ops:
  0.6 100.3 %shard_map.66 = (f32[752,1504]{1,0:T(8,128)S(1)}, f32[50,2500]{1,0:T(8,128)S(1)}, f32[1,128]{1,0:T(1,128)S(1)}) custom-call(bf16[200,2500]{1,0:T(8,128)(2,1)} %bitcast.6, bf16[2500,1504]{1,0:T(8,128)(2,1)} %bitcast.5, bf16[1,1504,6016]{2,1,0:T(8,128)(2,1)} %refs_2_.1), custom_call_target="tpu_custom_call" | custom-call | tf_op jit(solution)/shard_map/pallas_call | solution.py:849
  101.0 2.9 %shard_map.67 = (f32[752,1504]{1,0:T(8,128)}, f32[50,2500]{1,0:T(8,128)}, f32[1,1]{1,0:T(1,128)}, f32[1,1]{1,0:T(1,128)}) custom-call(f32[752,1504]{1,0:T(8,128)S(1)} %get-tuple-element.11.exch, f32[50,2500]{1,0:T(8,128)S(1)} %get-tuple-element.12.back, f32[1,128]{1,0:T(1,128)S(1)} %get-tuple-element.13.sums), custom_call_target="tpu_custom_call" | custom-call | tf_op jit(solution)/shard_map/pallas_call | solution.py:891

commit v5 on v4

--- a/solution.py
+++ b/solution.py
@@ -93,7 +93,7 @@
         return carry
 
     lax.fori_loop(1, size_x * size_y, hello, 0)
-    pl.semaphore_wait(barrier, size_x * size_y - 1)
+    return barrier
 
 
 def whole_kernel(g, names, *refs):
@@ -108,32 +108,41 @@
         remote(ref, ref, sem, r.spare, partner).wait_send()
 
     loads = [pltpu.make_async_copy(r.orb_h, r.orbv, r.load_sem.at[0])]
-    pieces = r.load_sem.shape[0] - 1
-    tall = up(-(-g.depth // pieces), 8)
-    for i in range(pieces):
-        low, high = i * tall, min((i + 1) * tall, g.depth)
-        loads.append(pltpu.make_async_copy(r.proj_h.at[low:high], r.projv.at[low:high], r.load_sem.at[i + 1]))
-    for load in loads:
-        load.start()
+    tail = (rows - 1) // g.lz
+
+    def piece_load(d, last_one):
+        low, high = tail * g.lz, rows
+        if not last_one:
+            low, high = pl.multiple_of(flip(z, d, nz) * g.lz, LANE), None
+        cut = pl.ds(low, g.lz if high is None else high - low)
+        return pltpu.make_async_copy(r.proj_h.at[:, cut], r.projv.at[:, cut], r.load_sem.at[d + 1])
+
+    def on_piece(d, act):
+        @pl.when(flip(z, d, nz) < tail)
+        def _():
+            act(piece_load(d, False))
+
+        @pl.when(flip(z, d, nz) == tail)
+        def _():
+            act(piece_load(d, True))
+
+    loads[0].start()
+    for d in reversed(range(nz)):
+        on_piece(d, lambda copy: copy.start())
     span = SUB * LANE
 
     def int_load(s):
         low, high = s * span, min((s + 1) * span, rows)
         return pltpu.make_async_copy(r.int_h.at[0, low:high], r.integ.at[low:high], r.int_sem.at[s])
 
-    greet(g.size_x, g.size_y)
-    for load in loads:
-        load.wait()
-    for s in range(g.subs):
-        int_load(s).start()
+    barrier = greet(g.size_x, g.size_y)
+    loads[0].wait()
 
     def x_part(zz, w, e):
         to = lax.rem(x + e, nx)
         return remote(
             r.part.at[zz, w, to], r.xland.at[e - 1, zz, w], r.send_p, r.recv_p.at[zz, w, e - 1], (z * nx + to, gy)
         )
-
-    tail = (rows - 1) // g.lz
 
     def put(zz, value):
         for w in range(g.waves):
@@ -144,6 +153,10 @@
 
     for d in reversed(range(nz)):
         zz = flip(z, d, nz)
+        on_piece(d, lambda copy: copy.wait())
+        if d == 0:
+            for s in range(g.subs):
+                int_load(s).start()
 
         @pl.when(zz < tail)
         def _(zz=zz):
@@ -153,6 +166,8 @@
         def _():
             put(tail, dot(r.orbv[...], r.projv[:, tail * g.lz:rows], ((1,), (0,))))
 
+        if d == nz - 1:
+            pl.semaphore_wait(barrier, g.size_x * g.size_y - 1)
         for w in range(g.waves):
             for e in range(1, nx):
                 x_part(zz, w, e).start()
@@ -316,12 +331,6 @@
             base = gg * rows + zz * g.lz
             for xx in range(nx):
                 r.admm[g.off[xx]:g.off[xx] + g.rx, base:base + width] = joined(gg, zz * nx + xx)[:, :width]
-    for zz in range(nz):
-        for xx in range(nx):
-            piece = joined(gy, zz * nx + xx)
-            piece = jnp.where(lane + zz * g.lz < rows, piece.astype(F32), 0.0).astype(BF16)
-            r.own[g.off[xx]:g.off[xx] + g.rx, zz * g.lz:(zz + 1) * g.lz] = piece
-
     devices = g.size_x * g.size_y
     me = gx * g.size_y + gy
     root = gx // g.per
@@ -382,8 +391,6 @@
                     row_y(q, unit, f).start()
                 row_c(q, unit).start()
 
-    r.mixed[...] = jnp.zeros_like(r.mixed)
-    r.trace[...] = jnp.zeros_like(r.trace)
     for s in range(g.subs):
         int_load(s).wait()
     spots = lax.broadcasted_iota(jnp.int32, (occ, span), 1)
@@ -426,9 +433,6 @@
                     row_y(gx, unit, f).start()
                 row_c(gx, unit).start()
 
-        exact = low.astype(F32)
-        r.trace[...] += jnp.sum(exact * exact, axis=0, keepdims=True)
-        r.mixed[...] += dot(r.own[:, pl.ds(start, span)], low, ((1,), (1,)))
         return carry
 
     lax.fori_loop(0, g.subs, half, 0)
@@ -451,7 +455,15 @@
                     pass_rows(z * nx + xx, g.na)
                 z_send(0, g.na + xx)
 
-    low = r.mixed[...].astype(BF16)
+    for zz in range(nz):
+        for xx in range(nx):
+            piece = joined(gy, zz * nx + xx)
+            piece = jnp.where(lane + zz * g.lz < rows, piece.astype(F32), 0.0).astype(BF16)
+            r.own[g.off[xx]:g.off[xx] + g.rx, zz * g.lz:(zz + 1) * g.lz] = piece
+    halves = jnp.concatenate([r.cols[gx, u] for u in range(g.units)], axis=1)
+    exact = halves.astype(F32)
+    r.trace[...] = jnp.sum(exact * exact, axis=0, keepdims=True)
+    low = dot(r.own[:, :g.wide], halves, ((1,), (1,))).astype(BF16)
     row_i = lax.broadcasted_iota(jnp.int32, (g.j, occ), 0)
     col_i = lax.broadcasted_iota(jnp.int32, (g.j, occ), 1)
     for gg in range(g.size_y):
@@ -509,18 +521,18 @@
     def units(ref, q, low, high):
         return jnp.concatenate([ref[q, u] for u in range(low, high)], axis=1)
 
+    def forward_rows(zz):
+        @pl.when(below)
+        def _():
+            for xx in range(nx):
+                row_came(zz * nx + xx).wait_recv()
+                row_all(zz * nx + xx).start()
+
     def exchange_term(zz):
-        for xx in range(nx):
-            q = zz * nx + xx
-
-            @pl.when(mine)
-            def _(q=q):
-                row_own(q).wait()
-
-            @pl.when(below)
-            def _(q=q):
-                row_came(q).wait_recv()
-                row_all(q).start()
+        @pl.when(mine)
+        def _():
+            for xx in range(nx):
+                row_own(zz * nx + xx).wait()
 
         @pl.when(last)
         def _():
@@ -661,6 +673,7 @@
 
     def work(k):
         if k < nz - 1:
+            level(k - 1, forward_rows)
             level(k - 1, exchange_term)
         else:
             for f in range(ny):
@@ -745,7 +758,10 @@
         back_c(n, 1 - c).start()
         if n > 0:
             back_on(n - 1)
+        if n == min(2, g.chunks - 1):
+            level(nz - 2, forward_rows)
     back_on(g.chunks - 1)
+    level(nz - 1, forward_rows)
     level(nz - 2, exchange_term)
     level(nz - 1, exchange_term)
     if g.odd:
@@ -802,9 +818,8 @@
         cols=vmem((g.size_x, g.units, occ, LANE), BF16),
         rows=vmem((g.size_x, g.wu, occ, LANE), BF16),
         acc=vmem((g.window, g.rows), F32),
-        mixed=vmem((occ, occ), F32),
         out_sem=dma(()),
-        trace=vmem((1, SUB * LANE), F32),
+        trace=vmem((1, g.wide), F32),
         mpart=vmem((g.size_y, g.j, occ), BF16),
         mland=vmem((g.size_y - 1, g.j, occ), BF16),
         mall=vmem((g.size_y, g.size_x, g.j, occ), BF16),
@@ -815,7 +830,7 @@
         bland=vmem((g.chunks, ny, g.j, g.step), BF16),
         bsum=vmem((g.chunks, ny, g.j, g.step), BF16),
         byland=vmem((g.chunks, ny - 1, g.j, g.step), BF16),
-        load_sem=dma((5,)),
+        load_sem=dma((nz + 1,)),
         int_sem=dma((g.subs,)),
         row_sem=dma((g.size_x,)),
     )

time: 105 us -> 103 us (0.981)
  Pallas kernels: 103 us -> 101 us
    pallas_call x1, Pallas kernels: 100 us -> 98.5 us  [whole(): pl.pallas_call(functools.partial(whole_kernel, g, names), out_shape=(vmem...]
where the time goes in v5:
time: 103 us; the launch traced here: 102 us
  Pallas kernels  101 us (98%)
    pallas_call x1, Pallas kernels, whole(): pl.pallas_call(functools.partial(whole_kernel, g, names), out_shape=(vmem...  98.5 us
    pallas_call x1, Pallas kernels, finish(): pl.pallas_call(functools.partial(finish_kernel, g), out_shape=(jax.ShapeD...  2.92 us

profile of v5, /device:TPU:21, one launch (start us, length us, event | category | flops | bytes accessed | tf_op | source)
XLA Modules:
  0.0 102.3 jit_solution(18410570282832942194)
XLA Ops:
  0.6 98.5 %shard_map.66 = (f32[752,1504]{1,0:T(8,128)S(1)}, f32[50,2500]{1,0:T(8,128)S(1)}, f32[1,128]{1,0:T(1,128)S(1)}) custom-call(bf16[200,2500]{1,0:T(8,128)(2,1)} %bitcast.6, bf16[2500,1504]{1,0:T(8,128)(2,1)} %bitcast.5, bf16[1,1504,6016]{2,1,0:T(8,128)(2,1)} %refs_2_.1), custom_call_target="tpu_custom_call" | custom-call | tf_op jit(solution)/shard_map/pallas_call | solution.py:864
  99.2 2.9 %shard_map.67 = (f32[752,1504]{1,0:T(8,128)}, f32[50,2500]{1,0:T(8,128)}, f32[1,1]{1,0:T(1,128)}, f32[1,1]{1,0:T(1,128)}) custom-call(f32[752,1504]{1,0:T(8,128)S(1)} %get-tuple-element.11.exch, f32[50,2500]{1,0:T(8,128)S(1)} %get-tuple-element.12.back, f32[1,128]{1,0:T(1,128)S(1)} %get-tuple-element.13.sums), custom_call_target="tpu_custom_call" | custom-call | tf_op jit(solution)/shard_map/pallas_call | solution.py:906
